TPU v7x, 256 devices: a whole 4x4x8 slice. The times are simulated.
256 devices in a mesh: rows: 256 (over x, y, z, core).
Axes of the slice: x: 4, y: 4, z: 8, core: 2. Of those that a mesh axis runs over, the one named last changes fastest.
Arguments:
- points: float32 [8, 1048576], P(None, 'rows'), may hold values from -6 to 6
- scales: float32 [8], replicated, may hold values from 1 to 3
- noise_var: float32 [1048576], P('rows'), may hold values from 0.05 to 0.5
- pivots: int32 [8, 16], replicated, may hold values from 0 to 1048575, as said below
Outputs:
- factor: float32 [128, 1048576], P(None, 'rows')
- residual_diag: float32 [1048576], P('rows')
- mean_residual: float32 [8], replicated
Inputs may be any that keep to these rules, and one draw needn't show every extreme that they name: `pivots`: all 128 entries are distinct point indices.
All inputs are finite; a program needn't handle non-finite values.
Results may differ from a plain program's by a relative error of at most 0.00014.
Values sent between devices are 32-bit elements; how exact they have to be, the bound alone decides.
No kernel may reach another device: no remote copies, remote signals or barrier semaphores. Data moves between devices by JAX's collectives and lax.ppermute only.
A program may use at most 64 MiB of HBM per device.

v0:
```python
import functools

import jax
import jax.numpy as jnp
from jax import lax
from jax.sharding import Mesh
from jax.sharding import PartitionSpec as P

ROWS = ("rows_0", "rows_1", "rows_2", "rows_3")


def by_axis(value, axes):
    return functools.reduce(lax.psum, axes, value)


def kernel(first_coords, second_coords):
    summed = jnp.zeros((first_coords.shape[1], second_coords.shape[1]), jnp.float32)
    for axis_pos in range(first_coords.shape[0]):
        differ = first_coords[axis_pos][:, None] - second_coords[axis_pos][None, :]
        summed = summed + differ * differ
    return jnp.exp(-0.5 * summed)


def pick_owned(values, wanted, offset):
    point_count = values.shape[-1]
    owned_mask = ((wanted >= offset) & (wanted < offset + point_count)).astype(jnp.float32)
    position = jnp.clip(wanted - offset, 0, point_count - 1)
    return jnp.take(values, position, axis=values.ndim - 1) * owned_mask


def body(points, scales, noise_var, pivots):
    point_count = points.shape[1]
    blocks, block_rows = pivots.shape
    rank_rows = blocks * block_rows
    total_points = point_count * lax.axis_size(ROWS)
    scaled = points / scales[:, None]
    offset = lax.axis_index(ROWS) * point_count
    local_ids = offset + lax.iota(jnp.int32, point_count)
    wanted_all = pivots.reshape(-1)
    coords_all, noise_all = (
        by_axis(pick_owned(scaled, wanted_all, offset), ROWS),
        by_axis(pick_owned(noise_var, wanted_all, offset), ROWS),
    )
    chol_all = jnp.linalg.cholesky(kernel(coords_all, coords_all) + jnp.diag(noise_all))

    def one_block(block_idx, state_tuple):
        factor, residual_diag, averages = state_tuple
        filled = block_idx * block_rows
        wanted = lax.dynamic_index_in_dim(pivots, block_idx, 0, keepdims=False)
        pivot_coords = lax.dynamic_slice_in_dim(coords_all, filled, block_rows, 1)
        band_rows = lax.dynamic_slice_in_dim(chol_all, filled, block_rows, 0)
        chol_block = lax.dynamic_slice_in_dim(band_rows, filled, block_rows, 1)
        update = jnp.einsum(
            "pr,rn->pn",
            band_rows,
            factor,
            precision=lax.Precision.HIGHEST,
            preferred_element_type=jnp.float32,
        )
        columns = kernel(pivot_coords, scaled) + jnp.where(
            local_ids[None, :] == wanted[:, None], noise_var[None, :], 0.0
        )
        columns = columns - update
        new_rows = lax.linalg.triangular_solve(chol_block, columns, left_side=True, lower=True)
        factor = lax.dynamic_update_slice_in_dim(factor, new_rows, filled, 0)
        residual_diag = residual_diag - jnp.sum(new_rows * new_rows, axis=0)
        local_sum = jnp.sum(residual_diag)
        averages = averages.at[block_idx].set(local_sum)
        return (factor, residual_diag, averages)

    start_state = (
        jnp.zeros((rank_rows, point_count), jnp.float32),
        1.0 + noise_var,
        jnp.zeros((blocks,), jnp.float32),
    )
    factor, residual_diag, averages = lax.fori_loop(0, blocks, one_block, start_state)
    averages = by_axis(averages, ROWS) / total_points
    return (factor, residual_diag, averages)


def solution(mesh):
    split = Mesh(mesh.devices.reshape(4, 4, 8, 2), ("rows_0", "rows_1", "rows_2", "rows_3"))
    return jax.shard_map(
        body,
        mesh=split,
        in_specs=(P(None, ROWS), P(), P(ROWS), P()),
        out_specs=(P(None, ROWS), P(ROWS), P()),
        check_vma=False,
    )
```

profile of v0, /device:TPU:1, one launch (start us, length us, event | category | flops | bytes accessed | tf_op | source)
XLA Modules:
  0.0 172.9 jit_solution(18299756232291610594)
XLA Ops:
  0.7 0.7 compare_and_fusion
  1.4 0.7 subtract_clamp_fusion
  2.2 1.6 gather_fusion.1
  4.0 2.8 %copy.10 = f32[8,4096]{0,1:T(8,128)} copy(f32[8,4096]{1,0:T(8,128)} %param.8) | data formatting | bytes 262144 | tf_op args[0]
  6.8 1.7 %broadcast_divide_fusion = f32[8,4096]{0,1:T(8,128)S(1)} fusion(f32[8,4096]{0,1:T(8,128)} %copy.10, f32[8]{0:T(128)S(1)} %copy-done.3), kind=kLoop, calls=%fused_computation.25 | loop fusion | flops 32768 | bytes 262176 | tf_op jit(solution)/shard_map/div | solution.py:36
  8.6 0.6 gather_fusion
  9.3 15.0 %all-reduce.2 = (f32[128]{0:T(128)S(1)}, f32[8,128]{0,1:T(8,128)S(1)}) all-reduce(f32[128]{0:T(128)S(1)} %get-tuple-element.379, f32[8,128]{0,1:T(8,128)S(1)} %multiply_bitcast_fusion), channel_id=1, replica_groups=mesh['rows_0'=4,'rows_1'=4,'rows_2'=8,'rows_3'=2] {'rows_0'}, use_global_device_ids=true, to_apply=%region_4.5 | all-reduce | flops 1152 | bytes 9216 | tf_op jit(solution)/shard_map/psum | solution.py:13
  24.3 14.4 %all-reduce.1 = (f32[128]{0:T(128)S(1)}, f32[8,128]{0,1:T(8,128)S(1)}) all-reduce(f32[128]{0:T(128)S(1)} %get-tuple-element.373, f32[8,128]{0,1:T(8,128)S(1)} %get-tuple-element.374), channel_id=1, replica_groups=mesh['rows_0'=4,'rows_1'=4,'rows_2'=8,'rows_3'=2] {'rows_1'}, use_global_device_ids=true, to_apply=%region_5.6 | all-reduce | flops 1152 | bytes 9216 | tf_op jit(solution)/shard_map/psum | solution.py:13
  38.7 26.4 %all-reduce = (f32[128]{0:T(128)S(1)}, f32[8,128]{0,1:T(8,128)S(1)}) all-reduce(f32[128]{0:T(128)S(1)} %get-tuple-element.371, f32[8,128]{0,1:T(8,128)S(1)} %get-tuple-element.372), channel_id=1, replica_groups=mesh['rows_0'=4,'rows_1'=4,'rows_2'=8,'rows_3'=2] {'rows_2'}, use_global_device_ids=true, to_apply=%region_6.7 | all-reduce | flops 1152 | bytes 9216 | tf_op jit(solution)/shard_map/psum | solution.py:13
  65.1 18.6 %all-reduce.3 = (f32[128]{0:T(128)S(1)}, f32[8,128]{0,1:T(8,128)S(1)}) all-reduce(f32[128]{0:T(128)S(1)} %get-tuple-element.369, f32[8,128]{0,1:T(8,128)S(1)} %get-tuple-element.370), channel_id=1, replica_groups=mesh['rows_0'=4,'rows_1'=4,'rows_2'=8,'rows_3'=2] {'rows_3'}, use_global_device_ids=true, to_apply=%region_7.8 | all-reduce | flops 1152 | bytes 9216 | tf_op jit(solution)/shard_map/psum | solution.py:13
  84.4 11.7 %cholesky.19 = f32[128,128]{1,0:T(8,128)S(1)} custom-call(f32[128,128]{1,0:T(8,128)S(1)} %add_multiply_fusion), custom_call_target="Cholesky" | custom-call | tf_op jit(solution)/shard_map/jit(cholesky)/cholesky | solution.py:44
  96.1 0.6 compare_reduce_fusion
  96.8 0.7 select_select_fusion
  97.5 0.6 copy.12
  98.3 42.2 %while.22 = (s32[]{:T(128)}, f32[128,4096]{1,0:T(8,128)S(1)}, f32[4096]{0:T(1024)S(1)}, f32[8]{0:T(128)S(1)}, f32[128,128]{1,0:T(8,128)S(1)}, /*index=5*/f32[8,1...) while((s32[]{:T(128)}, f32[128,4096]{1,0:T(8,128)S(1)}, ...), condition=%wide.region_13.14_spmd.clone, body=%wide.region_10.13_spmd.clone.sunk | while | flops 115221000 | bytes 3417037 | solution.py:76
  98.5 0.7 fusion.22
  99.2 1.2 convolution_subtract_fusion.2
  100.5 1.2 custom-call.20
  101.7 0.5 multiply_reduce_fusion.2
  102.2 0.6 fusion.23
  102.8 0.8 select_dynamic-update-slice_fusion.2
  103.8 0.7 fusion.22
  104.5 1.2 convolution_subtract_fusion.2
  105.7 1.2 custom-call.20
  107.4 0.6 fusion.23
  108.0 0.8 select_dynamic-update-slice_fusion.2
  109.0 0.7 fusion.22
  109.7 1.2 convolution_subtract_fusion.2
  111.0 1.2 custom-call.20
  112.2 0.5 multiply_reduce_fusion.2
  112.7 0.6 fusion.23
  113.3 0.8 select_dynamic-update-slice_fusion.2
  114.3 0.7 fusion.22
  115.0 1.2 convolution_subtract_fusion.2
  116.3 1.2 custom-call.20
  118.0 0.6 fusion.23
  118.6 0.8 select_dynamic-update-slice_fusion.2
  119.6 0.7 fusion.22
  120.3 1.2 convolution_subtract_fusion.2
  121.5 1.2 custom-call.20
  123.2 0.6 fusion.23
  123.8 0.8 select_dynamic-update-slice_fusion.2
  124.8 0.7 fusion.22
  125.5 1.2 convolution_subtract_fusion.2
  126.8 1.2 custom-call.20
  128.0 0.5 multiply_reduce_fusion.2
  128.5 0.6 fusion.23
  129.1 0.8 select_dynamic-update-slice_fusion.2
  130.1 0.7 fusion.22
  130.8 1.2 convolution_subtract_fusion.2
  132.1 1.2 custom-call.20
  133.8 0.6 fusion.23
  134.4 0.8 select_dynamic-update-slice_fusion.2
  135.4 0.7 fusion.22
  136.1 1.2 convolution_subtract_fusion.2
  137.3 1.2 custom-call.20
  138.6 0.5 multiply_reduce_fusion.2
  139.0 0.6 fusion.23
  139.6 0.8 select_dynamic-update-slice_fusion.2
  140.5 6.0 %psum.92 = f32[8]{0:T(128)S(1)} all-reduce(f32[8]{0:T(128)S(1)} %get-tuple-element.297), channel_id=1, replica_groups=mesh['rows_0'=4,'rows_1'=4,'rows_2'=8,'rows_3'=2] {'rows_0'}, use_global_device_ids=true, to_apply=%region_14.15 | all-reduce | flops 8 | bytes 64 | tf_op jit(solution)/shard_map/psum | solution.py:13
  146.5 6.0 %psum.93 = f32[8]{0:T(128)S(1)} all-reduce(f32[8]{0:T(128)S(1)} %psum.92), channel_id=1, replica_groups=mesh['rows_0'=4,'rows_1'=4,'rows_2'=8,'rows_3'=2] {'rows_1'}, use_global_device_ids=true, to_apply=%region_15.16 | all-reduce | flops 8 | bytes 64 | tf_op jit(solution)/shard_map/psum | solution.py:13
  152.4 11.0 %psum.94 = f32[8]{0:T(128)S(1)} all-reduce(f32[8]{0:T(128)S(1)} %psum.93), channel_id=1, replica_groups=mesh['rows_0'=4,'rows_1'=4,'rows_2'=8,'rows_3'=2] {'rows_2'}, use_global_device_ids=true, to_apply=%region_16.17 | all-reduce | flops 8 | bytes 64 | tf_op jit(solution)/shard_map/psum | solution.py:13
  163.4 8.9 %psum.95 = f32[8]{0:T(128)S(1)} all-reduce(f32[8]{0:T(128)S(1)} %psum.94), channel_id=1, replica_groups=mesh['rows_0'=4,'rows_1'=4,'rows_2'=8,'rows_3'=2] {'rows_3'}, use_global_device_ids=true, to_apply=%region_17.18 | all-reduce | flops 8 | bytes 64 | tf_op jit(solution)/shard_map/psum | solution.py:13
  172.3 0.5 broadcast_multiply_fusion
  (67 shorter events, 5.1 us)
Async XLA Ops:
  0.6 6.2 %copy-start.3 = (f32[8]{0:T(128)S(1)}, f32[8]{0:T(128)}, u32[]{:S(2)}) copy-start(f32[8]{0:T(128)} %param.9) | copy-start | bytes 100
  8.6 89.5 %copy-start.1 = (f32[4096]{0:T(1024)S(1)}, f32[4096]{0:T(1024)}, u32[]{:S(2)}) copy-start(f32[4096]{0:T(1024)} %param.10) | copy-start | bytes 49156
  140.5 32.4 %copy-start = (f32[128,4096]{1,0:T(8,128)}, f32[128,4096]{1,0:T(8,128)S(1)}, u32[]{:S(2)}) copy-start(f32[128,4096]{1,0:T(8,128)S(1)} %get-tuple-element.292) | copy-start | bytes 6291460
  140.5 32.4 %copy-start.2 = (f32[4096]{0:T(1024)}, f32[4096]{0:T(1024)S(1)}, u32[]{:S(2)}) copy-start(f32[4096]{0:T(1024)S(1)} %get-tuple-element.293) | copy-start | bytes 49156
where the time goes:
time: 174 us; the launch traced here: 173 us
  blocking collectives  106 us (61%)
  other arithmetic  39 us (22%)
  local copies, waits for them, and re-layouts  13.5 us (8%)
  matrix products  13.1 us (8%)
    psum x8, blocking collectives, by_axis(): return functools.reduce(lax.psum, axes, value)  106 us
    another operation x3, other arithmetic, body(): jnp.linalg.cholesky(kernel(coords_all, coords_all) + jnp.diag(noise_all))  12.4 us
    another operation x16, other arithmetic, one_block(): lax.linalg.triangular_solve(chol_block, columns, left_side=True, lower=True)  10.5 us
    dot_general x8, matrix products, one_block(): jnp.einsum('pr,rn->pn', band_rows, factor, precision=lax.Precision.HIGHES...  9.48 us
    scatter x8, other arithmetic, one_block(): averages = averages.at[block_idx].set(local_sum)  6.5 us
    eq x8, local copies, waits for them, and re-layouts, one_block(): local_ids[None, :] == wanted[:, None]  5.58 us
    reduce_sum x8, other arithmetic, one_block(): local_sum = jnp.sum(residual_diag)  4.9 us
    another operation x8, matrix products, one_block(): lax.linalg.triangular_solve(chol_block, columns, left_side=True, lower=True)  3.63 us

commit v1 on v0

v1 whole, which is shorter than its diff:
```python
import functools
import math

import jax
import jax.numpy as jnp
from jax import lax
from jax.experimental import pallas as pl
from jax.experimental.pallas import tpu as pltpu
from jax.sharding import Mesh
from jax.sharding import PartitionSpec as P

AXES = ("x", "y", "z", "c")
FIRST = ("x", "y", "c")
SECOND = ("z",)
LANES = 128
SUB = 8
ROOT = math.sqrt(0.5 * math.log2(math.e))
HIGH = lax.Precision.HIGHEST


def iota(shape, dim):
    return lax.broadcasted_iota(jnp.int32, shape, dim)


def splat_row(tile, row):
    return jnp.broadcast_to(tile[row : row + 1, :], tile.shape)


def splat_col(tile, col):
    return jnp.broadcast_to(tile[:, col : col + 1], tile.shape)


def local_pivots(pivots_ref, wide_ref, sizes, point_count):
    blocks, block_rows = pivots_ref.shape
    wide_ref[...] = jnp.zeros_like(wide_ref)
    wide_ref[:, 0:block_rows] = pivots_ref[...]
    lane = iota((SUB, LANES), 1)
    spread = jnp.take_along_axis(wide_ref[...], lane % block_rows, axis=1, mode="promise_in_bounds")
    row = jnp.zeros((SUB, LANES), jnp.int32)
    for block in range(blocks):
        row = jnp.where(lane // block_rows == block, splat_row(spread, block), row)
    index = lax.axis_index(AXES[0])
    for axis in AXES[1:]:
        index = index * sizes[axis] + lax.axis_index(axis)
    return row - index * point_count


def pre_kernel(sizes, copies, points_ref, noise_ref, scales_ref, pivots_ref, send_ref, scaled_ref, local_ref, wide_ref):
    dim, point_count = points_ref.shape
    tiles = point_count // LANES
    local = local_pivots(pivots_ref, wide_ref, sizes, point_count)
    local_ref[...] = local
    sub = iota((SUB, LANES), 0)
    scale = jnp.zeros((SUB, LANES), jnp.float32)
    for d in range(dim):
        scale = jnp.where(sub == d, scales_ref[d], scale)
    factor = ROOT / scale
    owned = (local >= 0) & (local < point_count)
    position = jnp.where(owned, local, -1)
    tile_of = position >> 7
    lane_of = position & (LANES - 1)
    coords = jnp.zeros((SUB, LANES), jnp.float32)
    for t in range(tiles):
        tile = points_ref[:, t * LANES : (t + 1) * LANES] * factor
        scaled_ref[:, t * LANES : (t + 1) * LANES] = tile
        found = jnp.take_along_axis(tile, lane_of, axis=1, mode="promise_in_bounds")
        coords = jnp.where(tile_of == t, found, coords)
    noise = jnp.zeros((SUB, LANES), jnp.float32)
    for a in range(tiles // SUB):
        found = jnp.take_along_axis(noise_ref[a * SUB : (a + 1) * SUB, :], lane_of, axis=1, mode="promise_in_bounds")
        noise = noise + jnp.where(tile_of == sub + a * SUB, found, 0.0)
    noise = jnp.sum(noise, axis=0, keepdims=True)
    for i in range(copies):
        send_ref[i * (dim + 1) : i * (dim + 1) + dim, :] = coords
        send_ref[i * (dim + 1) + dim : (i + 1) * (dim + 1), :] = noise


def main_kernel(
    block_rows, total, got_ref, scaled_ref, noise_ref, local_ref,
    out_ref, resid_ref, sums_ref, bcast_ref, pair_ref, cov_ref,
):
    dim, point_count = scaled_ref.shape
    rank = out_ref.shape[0]
    blocks = rank // block_rows
    halves = block_rows // SUB
    rows = dim + 1
    sub = iota((SUB, LANES), 0)
    lane = iota((SUB, LANES), 1)

    coords = got_ref[0:dim, :]
    noise_p = got_ref[dim:rows, :]
    for i in range(1, got_ref.shape[0] // rows):
        coords = coords + got_ref[i * rows : i * rows + dim, :]
        noise_p = noise_p + got_ref[i * rows + dim : (i + 1) * rows, :]
    local = local_ref[...].astype(jnp.float32)
    columns = jnp.transpose(jnp.concatenate([coords, local], axis=0))
    for d in range(rows):
        bcast_ref[d * rank : (d + 1) * rank, :] = jnp.broadcast_to(columns[:, d : d + 1], (rank, LANES))

    for g in range(rank // SUB):
        total_d = None
        for d in range(dim):
            diff = bcast_ref[d * rank + g * SUB : d * rank + (g + 1) * SUB, :] - splat_row(coords, d)
            total_d = diff * diff if total_d is None else total_d + diff * diff
        block = jnp.exp2(-total_d)
        block = block + jnp.where(lane == sub + g * SUB, jnp.broadcast_to(noise_p, (SUB, LANES)), 0.0)
        pair_ref[g * SUB : (g + 1) * SUB, :] = block

    for k in range(blocks):
        first = k * block_rows
        more = halves if k + 1 < blocks else 0
        tiles = [pair_ref[first + h * SUB : first + (h + 1) * SUB, :] for h in range(halves + more)]
        cols = [[splat_col(tile, first + j) for tile in tiles] for j in range(block_rows)]
        inside = (lane >= first) & (lane < first + block_rows)
        for h in range(halves + more):
            own = jnp.where(lane == sub + first + h * SUB, 1.0, 0.0)
            tiles[h] = jnp.where(inside, own if h < halves else 0.0, tiles[h])
        for m in range(block_rows):
            half, row = divmod(m, SUB)
            inv = lax.rsqrt(splat_row(cols[m][half], row))
            scaled_row = splat_row(tiles[half], row) * inv
            lower = [cols[m][h] * inv if h >= half else None for h in range(halves + more)]
            for j in range(m + 1, block_rows):
                half_j, row_j = divmod(j, SUB)
                entry = splat_row(lower[half_j], row_j)
                for h in range(half_j, halves + more):
                    cols[j][h] = cols[j][h] - lower[h] * entry
            for h in range(half, halves + more):
                if h == half:
                    below = tiles[h] - jnp.where(sub > row, lower[h], 0.0) * scaled_row
                    tiles[h] = jnp.where(sub == row, scaled_row, below)
                else:
                    tiles[h] = tiles[h] - lower[h] * scaled_row
        for h in range(halves + more):
            pair_ref[first + h * SUB : first + (h + 1) * SUB, :] = tiles[h]
        rest = first + 2 * block_rows
        if rest < rank:
            solved = jnp.concatenate(tiles[:halves], axis=0)
            left = jnp.transpose(solved)
            update = jnp.dot(left[rest:, :], solved, precision=HIGH, preferred_element_type=jnp.float32)
            lane_r = iota((rank - rest, LANES), 1)
            inside_r = (lane_r >= first) & (lane_r < first + block_rows)
            pair_ref[rest:, :] = jnp.where(inside_r, 0.0, pair_ref[rest:, :]) - update

    inverse = jnp.where(iota((rank, LANES), 1) <= iota((rank, LANES), 0), pair_ref[...], 0.0)

    width = 2 * LANES
    block_sums = [jnp.zeros((SUB, LANES), jnp.float32) for _ in range(blocks)]

    def step(t, block_sums):
        block_sums = list(block_sums)
        for u in range(width // LANES):
            at = pl.multiple_of(t * width + u * LANES, LANES)
            here = scaled_ref[:, pl.ds(at, LANES)]
            points_d = [splat_row(here, d) for d in range(dim)]
            noise_t = jnp.broadcast_to(noise_ref[pl.ds(t * (width // LANES) + u, 1), :], (SUB, LANES))
            ids = (lane + at).astype(jnp.float32)
            for g in range(rank // SUB):
                total_d = None
                for d in range(dim):
                    diff = bcast_ref[d * rank + g * SUB : d * rank + (g + 1) * SUB, :] - points_d[d]
                    total_d = diff * diff if total_d is None else total_d + diff * diff
                own = bcast_ref[dim * rank + g * SUB : dim * rank + (g + 1) * SUB, :] == ids
                cov_ref[g * SUB : (g + 1) * SUB, u * LANES : (u + 1) * LANES] = jnp.exp2(-total_d) + jnp.where(own, noise_t, 0.0)
        new = jnp.dot(inverse, cov_ref[...], precision=HIGH, preferred_element_type=jnp.float32)
        out_ref[:, pl.ds(pl.multiple_of(t * width, width), width)] = new
        for u in range(width // LANES):
            explained = None
            for b in range(blocks):
                part = None
                for h in range(halves):
                    at = b * block_rows + h * SUB
                    tile = new[at : at + SUB, u * LANES : (u + 1) * LANES]
                    part = tile * tile if part is None else part + tile * tile
                block_sums[b] = block_sums[b] + part
                explained = part if explained is None else explained + part
            row = t * (width // LANES) + u
            resid_ref[pl.ds(row, 1), :] = (1.0 + noise_ref[pl.ds(row, 1), :]) - jnp.sum(explained, axis=0, keepdims=True)
        return tuple(block_sums)

    block_sums = lax.fori_loop(0, point_count // width, step, tuple(block_sums))

    start = None
    for a in range(point_count // LANES // SUB):
        tile = 1.0 + noise_ref[a * SUB : (a + 1) * SUB, :]
        start = tile if start is None else start + tile
    running = start
    means = jnp.zeros((SUB, LANES), jnp.float32)
    for b in range(blocks):
        running = running - block_sums[b]
        means = jnp.where(sub == b, jnp.broadcast_to(jnp.sum(running, axis=0, keepdims=True), (SUB, LANES)), means)
    means = jnp.broadcast_to(jnp.sum(means, axis=1, keepdims=True), (SUB, LANES)) * (1.0 / total)
    sums_ref[...] = jnp.sum(jnp.where(sub == lane, means, 0.0), axis=0, keepdims=True)


def spread(value, axes, count):
    del count
    return lax.all_to_all(value, axes, 0, 0, tiled=False)


def body(sizes, points, scales, noise_var, pivots):
    dim, point_count = points.shape
    blocks, block_rows = pivots.shape
    rank = blocks * block_rows
    devices = math.prod(sizes.values())
    rows = dim + 1
    first = math.prod(sizes[a] for a in FIRST)
    second = math.prod(sizes[a] for a in SECOND)
    noise = noise_var.reshape(point_count // LANES, LANES)
    vmem = pl.BlockSpec(memory_space=pltpu.VMEM)
    smem = pl.BlockSpec(memory_space=pltpu.SMEM)
    send, scaled, local = pl.pallas_call(
        functools.partial(pre_kernel, sizes, first),
        out_shape=(
            jax.ShapeDtypeStruct((first * rows, LANES), jnp.float32),
            jax.ShapeDtypeStruct((dim, point_count), jnp.float32),
            jax.ShapeDtypeStruct((SUB, LANES), jnp.int32),
        ),
        in_specs=[vmem, vmem, smem, vmem],
        out_specs=(vmem, vmem, vmem),
        scratch_shapes=[pltpu.VMEM((SUB, LANES), jnp.int32)],
        name="pick_pivots",
    )(points, noise, scales, pivots)
    got = lax.all_to_all(send.reshape(first, rows, 1, LANES), FIRST, 0, 0)
    got = jnp.sum(got, axis=0)
    got = lax.all_to_all(jnp.broadcast_to(got[None], (second, rows, 1, LANES)), SECOND, 0, 0)
    factor, resid, sums = pl.pallas_call(
        functools.partial(main_kernel, block_rows, devices * point_count),
        out_shape=(
            jax.ShapeDtypeStruct((rank, point_count), jnp.float32),
            jax.ShapeDtypeStruct(noise.shape, jnp.float32),
            jax.ShapeDtypeStruct((1, LANES), jnp.float32),
        ),
        in_specs=[vmem] * 4,
        out_specs=(vmem,) * 3,
        scratch_shapes=[
            pltpu.VMEM((rows * rank, LANES), jnp.float32),
            pltpu.VMEM((rank, LANES), jnp.float32),
            pltpu.VMEM((rank, 2 * LANES), jnp.float32),
        ],
        name="factor_columns",
    )(got.reshape(second * rows, LANES), scaled, noise, local)
    parts = lax.all_to_all(jnp.broadcast_to(sums[None], (devices, 1, LANES)), AXES, 0, 0)
    means = jnp.sum(parts, axis=0)[0, :blocks]
    return factor, resid.reshape(point_count), means


def solution(mesh):
    split = Mesh(mesh.devices.reshape(4, 4, 8, 2), AXES)
    return jax.shard_map(
        functools.partial(body, dict(split.shape)),
        mesh=split,
        in_specs=(P(None, AXES), P(), P(AXES), P()),
        out_specs=(P(None, AXES), P(AXES), P()),
        check_vma=False,
    )
```

time: 174 us -> 67 us (0.39)
  blocking collectives: 106 us -> 51 us
  other arithmetic: 39 us -> 0.15 us
  Pallas kernels: 0 us -> 13.6 us
  matrix products: 13.1 us -> 0 us
  local copies, waits for them, and re-layouts: 13.5 us -> 1.26 us
    psum x8 -> x0, blocking collectives: 106 us -> none  [by_axis(): return functools.reduce(lax.psum, axes, value)]
    all_to_all x0 -> x3, blocking collectives: none -> 51 us  [the longest x1 19.5 us: body(): lax.all_to_all(jnp.broadcast_to(sums[None], (devices, 1, LANES)), AXES, 0...]
    another operation x19 -> x0, other arithmetic: 22.9 us -> none  [the longest x3 12.4 us: body(): jnp.linalg.cholesky(kernel(coords_all, coords_all) + jnp.diag(noise_all))]
    pallas_call x0 -> x2, Pallas kernels: none -> 13.6 us  [the longest x1 11.8 us: body(): pl.pallas_call(functools.partial(main_kernel, block_rows, devices * point...]
    dot_general x8 -> x0, matrix products: 9.48 us -> none  [one_block(): jnp.einsum('pr,rn->pn', band_rows, factor, precision=lax.Precision.HIGHES...]
    scatter x8 -> x0, other arithmetic: 6.5 us -> none  [one_block(): averages = averages.at[block_idx].set(local_sum)]
    eq x8 -> x0, local copies, waits for them, and re-layouts: 5.58 us -> none  [one_block(): local_ids[None, :] == wanted[:, None]]
    reduce_sum x8 -> x2, other arithmetic: 4.9 us -> 0.15 us  [the longest x1 0.1 us: body(): got = jnp.sum(got, axis=0)]
where the time goes in v1:
time: 67 us; the launch traced here: 66.7 us
  blocking collectives  51 us (76%)
  Pallas kernels  13.6 us (20%)
  local copies, waits for them, and re-layouts  1.26 us (2%)
    all_to_all x1, blocking collectives, body(): lax.all_to_all(jnp.broadcast_to(sums[None], (devices, 1, LANES)), AXES, 0...  19.5 us
    all_to_all x1, blocking collectives, body(): got = lax.all_to_all(send.reshape(first, rows, 1, LANES), FIRST, 0, 0)  16.4 us
    all_to_all x1, blocking collectives, body(): lax.all_to_all(jnp.broadcast_to(got[None], (second, rows, 1, LANES)), SEC...  15.1 us
    pallas_call x1, Pallas kernels, body(): pl.pallas_call(functools.partial(main_kernel, block_rows, devices * point...  11.8 us
    pallas_call x1, Pallas kernels, body(): pl.pallas_call(functools.partial(pre_kernel, sizes, first), out_shape=(ja...  1.8 us

profile of v1, /device:TPU:1, one launch (start us, length us, event | category | flops | bytes accessed | tf_op | source)
XLA Modules:
  0.0 66.7 jit_solution(14481568308748470450)
XLA Ops:
  0.6 1.8 %pick_pivots.1 = (f32[288,128]{1,0:T(8,128)}, f32[8,4096]{1,0:T(8,128)}, s32[8,128]{1,0:T(8,128)}) custom-call(f32[8,4096]{1,0:T(8,128)} %points_ref.1, f32[32,128]{1,0:T(8,128)} %bitcast.12, f32[8]{0:T(128)} %scales_ref.1, s32[8,16]{1,0:T(8,128)} %pivots_ref.1), custom_call_target="tpu_custom_call" | custom-call | tf_op jit(solution)/shard_map/pick_pivots/pallas_call | solution.py:212
  2.4 16.4 %all_to_all.15 = f32[32,9,1,128]{3,2,1,0:T(1,128)S(1)} all-to-all(f32[32,9,1,128]{3,2,1,0:T(1,128)} %bitcast.10), channel_id=1, replica_groups=mesh['x'=4,'y'=4,'z'=8,'c'=2] {'x','y','c'}, dimensions={0} | all-to-all | bytes 294912 | tf_op jit(solution)/shard_map/all_to_all | solution.py:224
  18.8 0.1 reduce_sum.20
  18.9 15.1 %all_to_all.16 = f32[8,9,1,128]{3,2,1,0:T(1,128)} all-to-all(f32[8,9,1,128]{3,2,1,0:T(1,128)S(1)} %broadcast_in_dim.6), channel_id=1, replica_groups=mesh['x'=4,'y'=4,'z'=8,'c'=2] {'z'}, dimensions={0} | all-to-all | bytes 73728 | tf_op jit(solution)/shard_map/all_to_all | solution.py:226
  34.0 11.8 %factor_columns.1 = (f32[128,4096]{1,0:T(8,128)}, f32[32,128]{1,0:T(8,128)}, f32[1,128]{1,0:T(1,128)}) custom-call(f32[72,128]{1,0:T(8,128)} %bitcast.11, f32[8,4096]{1,0:T(8,128)} %get-tuple-element.10.scaled_ref, f32[32,128]{1,0:T(8,128)} %bitcast.13, s32[8,128]{1,0:T(8,128)} %get-tuple-element.11.local_ref), custom_call_target="tpu_custom_call" | custom-call | tf_op jit(solution)/shard_map/factor_columns/pallas_call | solution.py:227
  45.9 0.7 %broadcast_in_dim.16 = f32[256,1,128]{2,1,0:T(1,128)S(1)} broadcast(f32[128]{0:T(128)} %bitcast.14), dimensions={2} | broadcast | bytes 131584 | tf_op jit(solution)/shard_map/broadcast_in_dim | solution.py:243
  46.6 19.5 %all_to_all.17 = f32[256,1,128]{2,1,0:T(1,128)S(1)} all-to-all(f32[256,1,128]{2,1,0:T(1,128)S(1)} %broadcast_in_dim.16), channel_id=1, replica_groups=mesh['x'=4,'y'=4,'z'=8,'c'=2] {'x','y','z','c'}, dimensions={0} | all-to-all | bytes 262144 | tf_op jit(solution)/shard_map/all_to_all | solution.py:243
  66.2 0.5 slice_bitcast_fusion
  (2 shorter events, 0.1 us)

commit v2 on v1

--- a/solution.py
+++ b/solution.py
@@ -45,7 +45,7 @@
     return row - index * point_count
 
 
-def pre_kernel(sizes, copies, points_ref, noise_ref, scales_ref, pivots_ref, send_ref, scaled_ref, local_ref, wide_ref):
+def pre_kernel(sizes, copies, points_ref, noise_ref, scales_ref, pivots_ref, send_ref, scaled_ref, local_ref, kept_ref, wide_ref):
     dim, point_count = points_ref.shape
     tiles = point_count // LANES
     local = local_pivots(pivots_ref, wide_ref, sizes, point_count)
@@ -65,6 +65,7 @@
         scaled_ref[:, t * LANES : (t + 1) * LANES] = tile
         found = jnp.take_along_axis(tile, lane_of, axis=1, mode="promise_in_bounds")
         coords = jnp.where(tile_of == t, found, coords)
+    kept_ref[...] = noise_ref[...]
     noise = jnp.zeros((SUB, LANES), jnp.float32)
     for a in range(tiles // SUB):
         found = jnp.take_along_axis(noise_ref[a * SUB : (a + 1) * SUB, :], lane_of, axis=1, mode="promise_in_bounds")
@@ -75,15 +76,27 @@
         send_ref[i * (dim + 1) + dim : (i + 1) * (dim + 1), :] = noise
 
 
+def covariance_tile(bcast_ref, scaled, noise_row, first_id, dim, rank, group, lane):
+    total = None
+    for d in range(dim):
+        at = d * rank + group * SUB
+        diff = bcast_ref[at : at + SUB, :] - scaled[d]
+        total = diff * diff if total is None else total + diff * diff
+    at = dim * rank + group * SUB
+    own = bcast_ref[at : at + SUB, :] == (lane + first_id).astype(jnp.float32)
+    return jnp.exp2(-total) + jnp.where(own, noise_row, 0.0)
+
+
 def main_kernel(
     block_rows, total, got_ref, scaled_ref, noise_ref, local_ref,
-    out_ref, resid_ref, sums_ref, bcast_ref, pair_ref, cov_ref,
+    out_hbm, resid_hbm, sums_ref, bcast_ref, pair_ref, cov_ref, out_ref, resid_ref, sems,
 ):
     dim, point_count = scaled_ref.shape
-    rank = out_ref.shape[0]
+    rank = pair_ref.shape[0]
     blocks = rank // block_rows
     halves = block_rows // SUB
     rows = dim + 1
+    tiles_n = point_count // LANES
     sub = iota((SUB, LANES), 0)
     lane = iota((SUB, LANES), 1)
 
@@ -133,6 +146,13 @@
                     tiles[h] = tiles[h] - lower[h] * scaled_row
         for h in range(halves + more):
             pair_ref[first + h * SUB : first + (h + 1) * SUB, :] = tiles[h]
+        for t in range(k * tiles_n // blocks, (k + 1) * tiles_n // blocks):
+            here = scaled_ref[:, t * LANES : (t + 1) * LANES]
+            scaled = [splat_row(here, d) for d in range(dim)]
+            noise_row = jnp.broadcast_to(noise_ref[t : t + 1, :], (SUB, LANES))
+            for g in range(rank // SUB):
+                tile = covariance_tile(bcast_ref, scaled, noise_row, t * LANES, dim, rank, g, lane)
+                cov_ref[g * SUB : (g + 1) * SUB, t * LANES : (t + 1) * LANES] = tile
         rest = first + 2 * block_rows
         if rest < rank:
             solved = jnp.concatenate(tiles[:halves], axis=0)
@@ -146,24 +166,14 @@
 
     width = 2 * LANES
     block_sums = [jnp.zeros((SUB, LANES), jnp.float32) for _ in range(blocks)]
-
-    def step(t, block_sums):
-        block_sums = list(block_sums)
-        for u in range(width // LANES):
-            at = pl.multiple_of(t * width + u * LANES, LANES)
-            here = scaled_ref[:, pl.ds(at, LANES)]
-            points_d = [splat_row(here, d) for d in range(dim)]
-            noise_t = jnp.broadcast_to(noise_ref[pl.ds(t * (width // LANES) + u, 1), :], (SUB, LANES))
-            ids = (lane + at).astype(jnp.float32)
-            for g in range(rank // SUB):
-                total_d = None
-                for d in range(dim):
-                    diff = bcast_ref[d * rank + g * SUB : d * rank + (g + 1) * SUB, :] - points_d[d]
-                    total_d = diff * diff if total_d is None else total_d + diff * diff
-                own = bcast_ref[dim * rank + g * SUB : dim * rank + (g + 1) * SUB, :] == ids
-                cov_ref[g * SUB : (g + 1) * SUB, u * LANES : (u + 1) * LANES] = jnp.exp2(-total_d) + jnp.where(own, noise_t, 0.0)
-        new = jnp.dot(inverse, cov_ref[...], precision=HIGH, preferred_element_type=jnp.float32)
-        out_ref[:, pl.ds(pl.multiple_of(t * width, width), width)] = new
+    copies = []
+    for t in range(point_count // width):
+        cols_t = slice(t * width, (t + 1) * width)
+        new = jnp.dot(inverse, cov_ref[:, cols_t], precision=HIGH, preferred_element_type=jnp.float32)
+        out_ref[:, cols_t] = new
+        copy = pltpu.make_async_copy(out_ref.at[:, cols_t], out_hbm.at[:, cols_t], sems.at[t])
+        copy.start()
+        copies.append(copy)
         for u in range(width // LANES):
             explained = None
             for b in range(blocks):
@@ -175,27 +185,23 @@
                 block_sums[b] = block_sums[b] + part
                 explained = part if explained is None else explained + part
             row = t * (width // LANES) + u
-            resid_ref[pl.ds(row, 1), :] = (1.0 + noise_ref[pl.ds(row, 1), :]) - jnp.sum(explained, axis=0, keepdims=True)
-        return tuple(block_sums)
-
-    block_sums = lax.fori_loop(0, point_count // width, step, tuple(block_sums))
-
-    start = None
-    for a in range(point_count // LANES // SUB):
+            resid_ref[row : row + 1, :] = (1.0 + noise_ref[row : row + 1, :]) - jnp.sum(explained, axis=0, keepdims=True)
+    copy = pltpu.make_async_copy(resid_ref, resid_hbm, sems.at[point_count // width])
+    copy.start()
+    copies.append(copy)
+
+    running = None
+    for a in range(tiles_n // SUB):
         tile = 1.0 + noise_ref[a * SUB : (a + 1) * SUB, :]
-        start = tile if start is None else start + tile
-    running = start
+        running = tile if running is None else running + tile
     means = jnp.zeros((SUB, LANES), jnp.float32)
     for b in range(blocks):
         running = running - block_sums[b]
         means = jnp.where(sub == b, jnp.broadcast_to(jnp.sum(running, axis=0, keepdims=True), (SUB, LANES)), means)
     means = jnp.broadcast_to(jnp.sum(means, axis=1, keepdims=True), (SUB, LANES)) * (1.0 / total)
-    sums_ref[...] = jnp.sum(jnp.where(sub == lane, means, 0.0), axis=0, keepdims=True)
-
-
-def spread(value, axes, count):
-    del count
-    return lax.all_to_all(value, axes, 0, 0, tiled=False)
+    sums_ref[...] = jnp.broadcast_to(jnp.sum(jnp.where(sub == lane, means, 0.0), axis=0, keepdims=True), sums_ref.shape)
+    for copy in copies:
+        copy.wait()
 
 
 def body(sizes, points, scales, noise_var, pivots):
@@ -209,15 +215,16 @@
     noise = noise_var.reshape(point_count // LANES, LANES)
     vmem = pl.BlockSpec(memory_space=pltpu.VMEM)
     smem = pl.BlockSpec(memory_space=pltpu.SMEM)
-    send, scaled, local = pl.pallas_call(
+    send, scaled, local, kept = pl.pallas_call(
         functools.partial(pre_kernel, sizes, first),
         out_shape=(
-            jax.ShapeDtypeStruct((first * rows, LANES), jnp.float32),
-            jax.ShapeDtypeStruct((dim, point_count), jnp.float32),
-            jax.ShapeDtypeStruct((SUB, LANES), jnp.int32),
+            pltpu.VMEM((first * rows, LANES), jnp.float32),
+            pltpu.VMEM((dim, point_count), jnp.float32),
+            pltpu.VMEM((SUB, LANES), jnp.int32),
+            pltpu.VMEM(noise.shape, jnp.float32),
         ),
         in_specs=[vmem, vmem, smem, vmem],
-        out_specs=(vmem, vmem, vmem),
+        out_specs=(vmem,) * 4,
         scratch_shapes=[pltpu.VMEM((SUB, LANES), jnp.int32)],
         name="pick_pivots",
     )(points, noise, scales, pivots)
@@ -229,18 +236,21 @@
         out_shape=(
             jax.ShapeDtypeStruct((rank, point_count), jnp.float32),
             jax.ShapeDtypeStruct(noise.shape, jnp.float32),
-            jax.ShapeDtypeStruct((1, LANES), jnp.float32),
+            pltpu.VMEM((devices, LANES), jnp.float32),
         ),
         in_specs=[vmem] * 4,
-        out_specs=(vmem,) * 3,
+        out_specs=(pl.BlockSpec(memory_space=pl.ANY),) * 2 + (vmem,),
         scratch_shapes=[
             pltpu.VMEM((rows * rank, LANES), jnp.float32),
             pltpu.VMEM((rank, LANES), jnp.float32),
-            pltpu.VMEM((rank, 2 * LANES), jnp.float32),
+            pltpu.VMEM((rank, point_count), jnp.float32),
+            pltpu.VMEM((rank, point_count), jnp.float32),
+            pltpu.VMEM(noise.shape, jnp.float32),
+            pltpu.SemaphoreType.DMA((point_count // (2 * LANES) + 1,)),
         ],
         name="factor_columns",
-    )(got.reshape(second * rows, LANES), scaled, noise, local)
-    parts = lax.all_to_all(jnp.broadcast_to(sums[None], (devices, 1, LANES)), AXES, 0, 0)
+    )(*(pltpu.with_memory_space_constraint(v, pltpu.VMEM) for v in (got.reshape(second * rows, LANES), scaled, kept, local)))
+    parts = lax.all_to_all(sums.reshape(devices, 1, LANES), AXES, 0, 0)
     means = jnp.sum(parts, axis=0)[0, :blocks]
     return factor, resid.reshape(point_count), means
 

time: 67 us -> 60.3 us (0.90)
  Pallas kernels: 13.6 us -> 7.8 us
  local copies, waits for them, and re-layouts: 1.26 us -> 0.54 us
    pallas_call x1, Pallas kernels: 11.8 us -> 6.67 us  [body(): pl.pallas_call(functools.partial(main_kernel, block_rows, devices * point...]
    broadcast_in_dim x1 -> x0, local copies, waits for them, and re-layouts: 0.72 us -> none  [body(): jnp.broadcast_to(sums[None], (devices, 1, LANES))]
where the time goes in v2:
time: 60.3 us; the launch traced here: 60.1 us
  blocking collectives  50.7 us (84%)
  Pallas kernels  7.8 us (13%)
  between operations  0.66 us (1%)
    all_to_all x1, blocking collectives, body(): parts = lax.all_to_all(sums.reshape(devices, 1, LANES), AXES, 0, 0)  19.5 us
    all_to_all x1, blocking collectives, body(): got = lax.all_to_all(send.reshape(first, rows, 1, LANES), FIRST, 0, 0)  16.2 us
    all_to_all x1, blocking collectives, body(): lax.all_to_all(jnp.broadcast_to(got[None], (second, rows, 1, LANES)), SEC...  15 us
    pallas_call x1, Pallas kernels, body(): pl.pallas_call(functools.partial(main_kernel, block_rows, devices * point...  6.67 us

profile of v2, /device:TPU:1, one launch (start us, length us, event | category | flops | bytes accessed | tf_op | source)
XLA Modules:
  0.0 60.1 jit_solution(15134970673520859030)
XLA Ops:
  0.6 1.1 %pick_pivots.1 = (f32[288,128]{1,0:T(8,128)S(1)}, f32[8,4096]{1,0:T(8,128)S(1)}, s32[8,128]{1,0:T(8,128)S(1)}, f32[32,128]{1,0:T(8,128)S(1)}) custom-call(f32[8,4096]{1,0:T(8,128)} %points_ref.1, f32[32,128]{1,0:T(8,128)} %bitcast.13, f32[8]{0:T(128)} %scales_ref.1, s32[8,16]{1,0:T(8,128)} %pivots_ref.1), custom_call_target="tpu_custom_call" | custom-call | tf_op jit(solution)/shard_map/pick_pivots/pallas_call | solution.py:218
  1.8 16.2 %all_to_all.15 = f32[32,9,1,128]{3,2,1,0:T(1,128)S(1)} all-to-all(f32[32,9,1,128]{3,2,1,0:T(1,128)S(1)} %bitcast.10), channel_id=1, replica_groups=mesh['x'=4,'y'=4,'z'=8,'c'=2] {'x','y','c'}, dimensions={0} | all-to-all | bytes 294912 | tf_op jit(solution)/shard_map/all_to_all | solution.py:231
  18.0 0.1 reduce_sum.20
  18.1 15.0 %all_to_all.16 = f32[8,9,1,128]{3,2,1,0:T(1,128)S(1)} all-to-all(f32[8,9,1,128]{3,2,1,0:T(1,128)S(1)} %broadcast_in_dim.2), channel_id=1, replica_groups=mesh['x'=4,'y'=4,'z'=8,'c'=2] {'z'}, dimensions={0} | all-to-all | bytes 73728 | tf_op jit(solution)/shard_map/all_to_all | solution.py:233
  33.1 6.7 %factor_columns.1 = (f32[128,4096]{1,0:T(8,128)}, f32[32,128]{1,0:T(8,128)}, f32[256,128]{1,0:T(8,128)S(1)}) custom-call(f32[72,128]{1,0:T(8,128)S(1)} %bitcast.11, f32[8,4096]{1,0:T(8,128)S(1)} %get-tuple-element.11.scaled_ref, f32[32,128]{1,0:T(8,128)S(1)} %get-tuple-element.12.noise_ref, s32[8,128]{1,0:T(8,128)S(1)} %get-tuple-element.13.local_ref), custom_call_target="tpu_custom_call" | custom-call | tf_op jit(solution)/shard_map/factor_columns/pallas_call | solution.py:234
  39.8 19.5 %all_to_all.17 = f32[256,1,128]{2,1,0:T(1,128)S(1)} all-to-all(f32[256,1,128]{2,1,0:T(1,128)S(1)} %bitcast.12), channel_id=1, replica_groups=mesh['x'=4,'y'=4,'z'=8,'c'=2] {'x','y','z','c'}, dimensions={0} | all-to-all | bytes 262144 | tf_op jit(solution)/shard_map/all_to_all | solution.py:253
  59.3 0.3 reduce_sum.21
  59.6 0.5 slice_bitcast_fusion
  (1 shorter events, 0.0 us)

commit v3 on v2

--- a/solution.py
+++ b/solution.py
@@ -10,12 +10,13 @@
 from jax.sharding import PartitionSpec as P
 
 AXES = ("x", "y", "z", "c")
-FIRST = ("x", "y", "c")
-SECOND = ("z",)
+GATHER = (("x", "y"), ("z", "c"))
+REDUCE = (("c",), ("x", "y", "z"))
 LANES = 128
 SUB = 8
 ROOT = math.sqrt(0.5 * math.log2(math.e))
 HIGH = lax.Precision.HIGHEST
+GRID = 16.0
 
 
 def iota(shape, dim):
@@ -76,20 +77,59 @@
         send_ref[i * (dim + 1) + dim : (i + 1) * (dim + 1), :] = noise
 
 
-def covariance_tile(bcast_ref, scaled, noise_row, first_id, dim, rank, group, lane):
-    total = None
-    for d in range(dim):
-        at = d * rank + group * SUB
-        diff = bcast_ref[at : at + SUB, :] - scaled[d]
-        total = diff * diff if total is None else total + diff * diff
-    at = dim * rank + group * SUB
-    own = bcast_ref[at : at + SUB, :] == (lane + first_id).astype(jnp.float32)
-    return jnp.exp2(-total) + jnp.where(own, noise_row, 0.0)
+def pieces(value):
+    high = value.astype(jnp.bfloat16)
+    value = value - high.astype(jnp.float32)
+    middle = value.astype(jnp.bfloat16)
+    return high, middle, (value - middle.astype(jnp.float32)).astype(jnp.bfloat16)
+
+
+def features(coords, second):
+    dim, count = coords.shape
+    sub = iota((SUB, count), 0)
+    coarse = jnp.round(coords * GRID)
+    near = coarse * (1.0 / GRID)
+    rest = coords - near
+    low1 = rest.astype(jnp.bfloat16).astype(jnp.float32)
+    left = rest - low1
+    low2 = left.astype(jnp.bfloat16).astype(jnp.float32)
+    low3 = left - low2
+    square = jnp.sum(coarse * coarse, axis=0, keepdims=True)
+    square_high = jnp.floor(square * (1.0 / 256)) * 256.0
+    square_low = square - square_high
+    mixed = jnp.sum(rest * (coords + near), axis=0, keepdims=True)
+    mixed1 = mixed.astype(jnp.bfloat16).astype(jnp.float32)
+    mixed2 = (mixed - mixed1).astype(jnp.bfloat16).astype(jnp.float32)
+    mixed3 = mixed - mixed1 - mixed2
+
+    def rows(*values):
+        group = jnp.zeros((SUB, count), jnp.float32)
+        for i, value in enumerate(values):
+            group = jnp.where(sub == i, value, group)
+        return group
+
+    if second:
+        return (
+            coarse, rows(1.0, 1.0, square_high, square_low),
+            low1, low2, low3, low1, low2, low1, near, near, near, rows(1.0, 1.0, 1.0, mixed1, mixed2, mixed3),
+        )
+    unit = -1.0 / (GRID * GRID)
+    two = 2.0 * near
+    return (
+        coarse * (-2.0 * unit), rows(square_high * unit, square_low * unit, unit, unit),
+        two, two, two, 2.0 * low1, 2.0 * low1, 2.0 * low2, 2.0 * low1, 2.0 * low2, 2.0 * low3,
+        rows(-mixed1, -mixed2, -mixed3, -1.0, -1.0, -1.0),
+    )
+
+
+def exponent(left, right):
+    coarse = jnp.dot(left[:, : 2 * SUB], right[: 2 * SUB, :], preferred_element_type=jnp.float32)
+    return coarse + jnp.dot(left[:, 2 * SUB :], right[2 * SUB :, :], preferred_element_type=jnp.float32)
 
 
 def main_kernel(
     block_rows, total, got_ref, scaled_ref, noise_ref, local_ref,
-    out_hbm, resid_hbm, sums_ref, bcast_ref, pair_ref, cov_ref, out_ref, resid_ref, sems,
+    out_hbm, resid_hbm, sums_ref, side_ref, pair_ref, cov_ref, out_ref, resid_ref, sems,
 ):
     dim, point_count = scaled_ref.shape
     rank = pair_ref.shape[0]
@@ -97,6 +137,7 @@
     halves = block_rows // SUB
     rows = dim + 1
     tiles_n = point_count // LANES
+    width = 2 * LANES
     sub = iota((SUB, LANES), 0)
     lane = iota((SUB, LANES), 1)
 
@@ -106,18 +147,18 @@
         coords = coords + got_ref[i * rows : i * rows + dim, :]
         noise_p = noise_p + got_ref[i * rows + dim : (i + 1) * rows, :]
     local = local_ref[...].astype(jnp.float32)
-    columns = jnp.transpose(jnp.concatenate([coords, local], axis=0))
-    for d in range(rows):
-        bcast_ref[d * rank : (d + 1) * rank, :] = jnp.broadcast_to(columns[:, d : d + 1], (rank, LANES))
-
-    for g in range(rank // SUB):
-        total_d = None
-        for d in range(dim):
-            diff = bcast_ref[d * rank + g * SUB : d * rank + (g + 1) * SUB, :] - splat_row(coords, d)
-            total_d = diff * diff if total_d is None else total_d + diff * diff
-        block = jnp.exp2(-total_d)
-        block = block + jnp.where(lane == sub + g * SUB, jnp.broadcast_to(noise_p, (SUB, LANES)), 0.0)
-        pair_ref[g * SUB : (g + 1) * SUB, :] = block
+    wanted = jnp.broadcast_to(jnp.transpose(local)[:, :1], (rank, LANES))
+    pivot_side = jnp.transpose(jnp.concatenate(features(coords, False), axis=0)).astype(jnp.bfloat16)
+    own_side = jnp.concatenate(features(coords, True), axis=0).astype(jnp.bfloat16)
+
+    same = iota((rank, LANES), 0) == iota((rank, LANES), 1)
+    pair_ref[...] = jnp.where(same, 1.0 + noise_p, jnp.exp2(exponent(pivot_side, own_side)))
+
+    for t in range(tiles_n):
+        groups = features(scaled_ref[:, t * LANES : (t + 1) * LANES], True)
+        for i in range(0, len(groups), 2):
+            pair = jnp.concatenate(groups[i : i + 2], axis=0).astype(jnp.bfloat16)
+            side_ref[i * SUB : (i + 2) * SUB, t * LANES : (t + 1) * LANES] = pair
 
     for k in range(blocks):
         first = k * block_rows
@@ -146,30 +187,36 @@
                     tiles[h] = tiles[h] - lower[h] * scaled_row
         for h in range(halves + more):
             pair_ref[first + h * SUB : first + (h + 1) * SUB, :] = tiles[h]
-        for t in range(k * tiles_n // blocks, (k + 1) * tiles_n // blocks):
-            here = scaled_ref[:, t * LANES : (t + 1) * LANES]
-            scaled = [splat_row(here, d) for d in range(dim)]
-            noise_row = jnp.broadcast_to(noise_ref[t : t + 1, :], (SUB, LANES))
-            for g in range(rank // SUB):
-                tile = covariance_tile(bcast_ref, scaled, noise_row, t * LANES, dim, rank, g, lane)
-                cov_ref[g * SUB : (g + 1) * SUB, t * LANES : (t + 1) * LANES] = tile
+        for t in range(k * tiles_n // blocks, (k + 1) * tiles_n // blocks, width // LANES):
+            power = exponent(pivot_side, side_ref[:, t * LANES : t * LANES + width])
+            for u in range(width // LANES):
+                noisy = 1.0 + noise_ref[t + u : t + u + 1, :]
+                ids = (iota((rank, LANES), 1) + (t + u) * LANES).astype(jnp.float32)
+                tile = jnp.where(wanted == ids, noisy, jnp.exp2(power[:, u * LANES : (u + 1) * LANES]))
+                high, middle, low = pieces(tile)
+                for i, piece in enumerate((middle, high, low)):
+                    cov_ref[i * rank : (i + 1) * rank, (t + u) * LANES : (t + u + 1) * LANES] = piece
         rest = first + 2 * block_rows
         if rest < rank:
             solved = jnp.concatenate(tiles[:halves], axis=0)
-            left = jnp.transpose(solved)
-            update = jnp.dot(left[rest:, :], solved, precision=HIGH, preferred_element_type=jnp.float32)
+            high, middle, low = (piece.astype(jnp.float32) for piece in pieces(solved))
+            turned = jnp.transpose(jnp.concatenate([high, high, middle, middle, low, high], axis=0)).astype(jnp.bfloat16)
+            flat = jnp.concatenate([high, middle, high, middle, high, low], axis=0).astype(jnp.bfloat16)
+            update = jnp.dot(turned[rest:, :], flat, preferred_element_type=jnp.float32)
             lane_r = iota((rank - rest, LANES), 1)
             inside_r = (lane_r >= first) & (lane_r < first + block_rows)
             pair_ref[rest:, :] = jnp.where(inside_r, 0.0, pair_ref[rest:, :]) - update
 
     inverse = jnp.where(iota((rank, LANES), 1) <= iota((rank, LANES), 0), pair_ref[...], 0.0)
 
-    width = 2 * LANES
+    high, middle, low = pieces(inverse)
+    left = jnp.concatenate([high, high, middle, middle, low, high], axis=1)
     block_sums = [jnp.zeros((SUB, LANES), jnp.float32) for _ in range(blocks)]
     copies = []
     for t in range(point_count // width):
         cols_t = slice(t * width, (t + 1) * width)
-        new = jnp.dot(inverse, cov_ref[:, cols_t], precision=HIGH, preferred_element_type=jnp.float32)
+        large, small = cov_ref[: 2 * rank, cols_t], cov_ref[rank:, cols_t]
+        new = jnp.dot(left, jnp.concatenate([large, large, small], axis=0), preferred_element_type=jnp.float32)
         out_ref[:, cols_t] = new
         copy = pltpu.make_async_copy(out_ref.at[:, cols_t], out_hbm.at[:, cols_t], sems.at[t])
         copy.start()
@@ -204,21 +251,63 @@
         copy.wait()
 
 
+def exchange(stacked, groups, sizes):
+    for i, group in enumerate(groups):
+        if i > 0:
+            value = jnp.sum(stacked, axis=0)
+            stacked = jnp.broadcast_to(value[None], (group_size(group, sizes),) + value.shape)
+        if group == ("c",):
+            other = lax.ppermute(stacked[0], "c", ((0, 1), (1, 0)))
+            stacked = jnp.stack([stacked[0], other])
+        else:
+            stacked = lax.all_to_all(stacked, group, 0, 0)
+    return stacked
+
+
+def group_size(group, sizes):
+    return math.prod(sizes[axis] for axis in group)
+
+
+def factor_call(block_rows, total, sum_copies, got, scaled, kept, local):
+    point_count = scaled.shape[1]
+    rank = local.shape[1]
+    vmem = pl.BlockSpec(memory_space=pltpu.VMEM)
+    hbm = pl.BlockSpec(memory_space=pl.ANY)
+    return pl.pallas_call(
+        functools.partial(main_kernel, block_rows, total),
+        out_shape=(
+            jax.ShapeDtypeStruct((rank, point_count), jnp.float32),
+            jax.ShapeDtypeStruct(kept.shape, jnp.float32),
+            pltpu.VMEM((sum_copies, LANES), jnp.float32),
+        ),
+        in_specs=[vmem] * 4,
+        out_specs=(hbm, hbm, vmem),
+        scratch_shapes=[
+            pltpu.VMEM((12 * SUB, point_count), jnp.bfloat16),
+            pltpu.VMEM((rank, LANES), jnp.float32),
+            pltpu.VMEM((3 * rank, point_count), jnp.bfloat16),
+            pltpu.VMEM((rank, point_count), jnp.float32),
+            pltpu.VMEM(kept.shape, jnp.float32),
+            pltpu.SemaphoreType.DMA((point_count // (2 * LANES) + 1,)),
+        ],
+        name="factor_columns",
+    )(*(pltpu.with_memory_space_constraint(v, pltpu.VMEM) for v in (got, scaled, kept, local)))
+
+
 def body(sizes, points, scales, noise_var, pivots):
     dim, point_count = points.shape
     blocks, block_rows = pivots.shape
-    rank = blocks * block_rows
     devices = math.prod(sizes.values())
     rows = dim + 1
-    first = math.prod(sizes[a] for a in FIRST)
-    second = math.prod(sizes[a] for a in SECOND)
+    copies = group_size(GATHER[0], sizes)
+    sum_copies = group_size(REDUCE[0], sizes)
     noise = noise_var.reshape(point_count // LANES, LANES)
     vmem = pl.BlockSpec(memory_space=pltpu.VMEM)
     smem = pl.BlockSpec(memory_space=pltpu.SMEM)
     send, scaled, local, kept = pl.pallas_call(
-        functools.partial(pre_kernel, sizes, first),
+        functools.partial(pre_kernel, sizes, copies),
         out_shape=(
-            pltpu.VMEM((first * rows, LANES), jnp.float32),
+            pltpu.VMEM((copies * rows, LANES), jnp.float32),
             pltpu.VMEM((dim, point_count), jnp.float32),
             pltpu.VMEM((SUB, LANES), jnp.int32),
             pltpu.VMEM(noise.shape, jnp.float32),
@@ -228,29 +317,10 @@
         scratch_shapes=[pltpu.VMEM((SUB, LANES), jnp.int32)],
         name="pick_pivots",
     )(points, noise, scales, pivots)
-    got = lax.all_to_all(send.reshape(first, rows, 1, LANES), FIRST, 0, 0)
-    got = jnp.sum(got, axis=0)
-    got = lax.all_to_all(jnp.broadcast_to(got[None], (second, rows, 1, LANES)), SECOND, 0, 0)
-    factor, resid, sums = pl.pallas_call(
-        functools.partial(main_kernel, block_rows, devices * point_count),
-        out_shape=(
-            jax.ShapeDtypeStruct((rank, point_count), jnp.float32),
-            jax.ShapeDtypeStruct(noise.shape, jnp.float32),
-            pltpu.VMEM((devices, LANES), jnp.float32),
-        ),
-        in_specs=[vmem] * 4,
-        out_specs=(pl.BlockSpec(memory_space=pl.ANY),) * 2 + (vmem,),
-        scratch_shapes=[
-            pltpu.VMEM((rows * rank, LANES), jnp.float32),
-            pltpu.VMEM((rank, LANES), jnp.float32),
-            pltpu.VMEM((rank, point_count), jnp.float32),
-            pltpu.VMEM((rank, point_count), jnp.float32),
-            pltpu.VMEM(noise.shape, jnp.float32),
-            pltpu.SemaphoreType.DMA((point_count // (2 * LANES) + 1,)),
-        ],
-        name="factor_columns",
-    )(*(pltpu.with_memory_space_constraint(v, pltpu.VMEM) for v in (got.reshape(second * rows, LANES), scaled, kept, local)))
-    parts = lax.all_to_all(sums.reshape(devices, 1, LANES), AXES, 0, 0)
+    got = exchange(send.reshape(copies, rows, 1, LANES), GATHER, sizes)
+    got = got.reshape(-1, LANES)
+    factor, resid, sums = factor_call(block_rows, devices * point_count, sum_copies, got, scaled, kept, local)
+    parts = exchange(sums.reshape(sum_copies, 1, LANES), REDUCE, sizes)
     means = jnp.sum(parts, axis=0)[0, :blocks]
     return factor, resid.reshape(point_count), means
 

time: 60.3 us -> 58.2 us (0.965)
  blocking collectives: 50.7 us -> 48.3 us
  waiting for transfers between devices: 0 us -> 1.05 us
  Pallas kernels: 7.8 us -> 7.1 us
    all_to_all x3, blocking collectives: 50.7 us -> 48.3 us  [exchange(): stacked = lax.all_to_all(stacked, group, 0, 0)]
    ppermute x0 -> x1, waiting for transfers between devices: none -> 1.05 us  [exchange(): other = lax.ppermute(stacked[0], 'c', ((0, 1), (1, 0)))]
    pallas_call x2, Pallas kernels: 7.8 us -> 7.1 us  [the longest x1 5.97 us: factor_call(): pl.pallas_call(functools.partial(main_kernel, block_rows, total), out_sha...]
  transfers between devices with their start and end apart: 0 -> 1, of which waited for: 0 -> 1; matrix products, arithmetic and copies ran while one was open for 0% -> 0% of each run, Pallas kernels for 0% -> 0%
where the time goes in v3:
time: 58.2 us; the launch traced here: 58 us
  blocking collectives  48.3 us (83%)
  Pallas kernels  7.1 us (12%)
  waiting for transfers between devices  1.05 us (2%)
  between operations  0.67 us (1%)
  local copies, waits for them, and re-layouts  0.6 us (1%)
    all_to_all x3, blocking collectives, exchange(): stacked = lax.all_to_all(stacked, group, 0, 0)  48.3 us
    pallas_call x1, Pallas kernels, factor_call(): pl.pallas_call(functools.partial(main_kernel, block_rows, total), out_sha...  5.97 us
  transfers between devices with their start and end apart: 1, of which 1 were waited for; matrix products, arithmetic and copies ran while one was open for 0% of the time, Pallas kernels for 0%

profile of v3, /device:TPU:1, one launch (start us, length us, event | category | flops | bytes accessed | tf_op | source)
XLA Modules:
  0.0 58.0 jit_solution(6880740367205402602)
XLA Ops:
  0.6 1.1 %pick_pivots.1 = (f32[144,128]{1,0:T(8,128)S(1)}, f32[8,4096]{1,0:T(8,128)S(1)}, s32[8,128]{1,0:T(8,128)S(1)}, f32[32,128]{1,0:T(8,128)S(1)}) custom-call(f32[8,4096]{1,0:T(8,128)} %points_ref.1, f32[32,128]{1,0:T(8,128)} %bitcast.13, f32[8]{0:T(128)} %scales_ref.1, s32[8,16]{1,0:T(8,128)} %pivots_ref.1), custom_call_target="tpu_custom_call" | custom-call | tf_op jit(solution)/shard_map/pick_pivots/pallas_call | solution.py:307
  1.8 13.9 %all_to_all.15 = f32[16,9,1,128]{3,2,1,0:T(1,128)S(1)} all-to-all(f32[16,9,1,128]{3,2,1,0:T(1,128)S(1)} %bitcast.11), channel_id=1, replica_groups=mesh['x'=4,'y'=4,'z'=8,'c'=2] {'x','y'}, dimensions={0} | all-to-all | bytes 147456 | tf_op jit(solution)/shard_map/all_to_all | solution.py:263
  15.7 0.1 reduce_sum.33
  15.8 18.3 %all_to_all.16 = f32[16,9,1,128]{3,2,1,0:T(1,128)S(1)} all-to-all(f32[16,9,1,128]{3,2,1,0:T(1,128)S(1)} %broadcast_in_dim.4), channel_id=1, replica_groups=mesh['x'=4,'y'=4,'z'=8,'c'=2] {'z','c'}, dimensions={0} | all-to-all | bytes 147456 | tf_op jit(solution)/shard_map/all_to_all | solution.py:263
  34.1 6.0 %factor_columns.1 = (f32[128,4096]{1,0:T(8,128)}, f32[32,128]{1,0:T(8,128)}, f32[2,128]{1,0:T(2,128)S(1)}) custom-call(f32[144,128]{1,0:T(8,128)S(1)} %bitcast.10, f32[8,4096]{1,0:T(8,128)S(1)} %get-tuple-element.11.scaled_ref, f32[32,128]{1,0:T(8,128)S(1)} %get-tuple-element.12.noise_ref, s32[8,128]{1,0:T(8,128)S(1)} %get-tuple-element.13.local_ref), custom_call_target="tpu_custom_call" | custom-call | tf_op jit(solution)/shard_map/factor_columns/pallas_call | solution.py:276
  40.1 0.2 collective-permute-start
  40.3 1.1 %collective-permute-done = f32[1,128]{1,0:T(1,128)S(1)} collective-permute-done((f32[1,128]{1,0:T(1,128)S(1)}, f32[1,128]{1,0:T(1,128)S(1)}, u32[]{:S(2)}, u32[]{:S(2)}) %collective-permute-start) | collective-permute-done | bytes 544 | tf_op jit(solution)/shard_map/ppermute | solution.py:260
  41.4 16.1 %all_to_all.17 = f32[128,1,128]{2,1,0:T(1,128)S(1)} all-to-all(f32[128,1,128]{2,1,0:T(1,128)S(1)} %broadcast_in_dim.5), channel_id=1, replica_groups=mesh['x'=4,'y'=4,'z'=8,'c'=2] {'x','y','z'}, dimensions={0} | all-to-all | bytes 131072 | tf_op jit(solution)/shard_map/all_to_all | solution.py:263
  57.5 0.5 slice_bitcast_fusion
  (5 shorter events, 0.1 us)
Async XLA Ops:
  40.1 1.2 %collective-permute-start = (f32[1,128]{1,0:T(1,128)S(1)}, f32[1,128]{1,0:T(1,128)S(1)}, u32[]{:S(2)}, u32[]{:S(2)}) collective-permute-start(f32[1,128]{1,0:T(1,128)S(1)} %slice.8), channel_id=1, source_target_pairs={{0,1},{1,0},{2,3},{3,2},{4,5},{5,4},{6,7},{7,6},{8,9},{9,8},{10,11... | collective-permute-start | bytes 1544 | tf_op jit(solution)/shard_map/ppermute | solution.py:260

commit v4 on v3

--- a/solution.py
+++ b/solution.py
@@ -129,7 +129,7 @@
 
 def main_kernel(
     block_rows, total, got_ref, scaled_ref, noise_ref, local_ref,
-    out_hbm, resid_hbm, sums_ref, side_ref, pair_ref, cov_ref, out_ref, resid_ref, sems,
+    out_ref, resid_ref, sums_ref, side_ref, pair_ref, cov_ref,
 ):
     dim, point_count = scaled_ref.shape
     rank = pair_ref.shape[0]
@@ -212,15 +212,11 @@
     high, middle, low = pieces(inverse)
     left = jnp.concatenate([high, high, middle, middle, low, high], axis=1)
     block_sums = [jnp.zeros((SUB, LANES), jnp.float32) for _ in range(blocks)]
-    copies = []
     for t in range(point_count // width):
         cols_t = slice(t * width, (t + 1) * width)
         large, small = cov_ref[: 2 * rank, cols_t], cov_ref[rank:, cols_t]
         new = jnp.dot(left, jnp.concatenate([large, large, small], axis=0), preferred_element_type=jnp.float32)
         out_ref[:, cols_t] = new
-        copy = pltpu.make_async_copy(out_ref.at[:, cols_t], out_hbm.at[:, cols_t], sems.at[t])
-        copy.start()
-        copies.append(copy)
         for u in range(width // LANES):
             explained = None
             for b in range(blocks):
@@ -233,9 +229,6 @@
                 explained = part if explained is None else explained + part
             row = t * (width // LANES) + u
             resid_ref[row : row + 1, :] = (1.0 + noise_ref[row : row + 1, :]) - jnp.sum(explained, axis=0, keepdims=True)
-    copy = pltpu.make_async_copy(resid_ref, resid_hbm, sems.at[point_count // width])
-    copy.start()
-    copies.append(copy)
 
     running = None
     for a in range(tiles_n // SUB):
@@ -247,8 +240,6 @@
         means = jnp.where(sub == b, jnp.broadcast_to(jnp.sum(running, axis=0, keepdims=True), (SUB, LANES)), means)
     means = jnp.broadcast_to(jnp.sum(means, axis=1, keepdims=True), (SUB, LANES)) * (1.0 / total)
     sums_ref[...] = jnp.broadcast_to(jnp.sum(jnp.where(sub == lane, means, 0.0), axis=0, keepdims=True), sums_ref.shape)
-    for copy in copies:
-        copy.wait()
 
 
 def exchange(stacked, groups, sizes):
@@ -272,26 +263,52 @@
     point_count = scaled.shape[1]
     rank = local.shape[1]
     vmem = pl.BlockSpec(memory_space=pltpu.VMEM)
-    hbm = pl.BlockSpec(memory_space=pl.ANY)
     return pl.pallas_call(
         functools.partial(main_kernel, block_rows, total),
         out_shape=(
-            jax.ShapeDtypeStruct((rank, point_count), jnp.float32),
-            jax.ShapeDtypeStruct(kept.shape, jnp.float32),
+            pltpu.VMEM((rank, point_count), jnp.float32),
+            pltpu.VMEM(kept.shape, jnp.float32),
             pltpu.VMEM((sum_copies, LANES), jnp.float32),
         ),
         in_specs=[vmem] * 4,
-        out_specs=(hbm, hbm, vmem),
+        out_specs=(vmem,) * 3,
         scratch_shapes=[
             pltpu.VMEM((12 * SUB, point_count), jnp.bfloat16),
             pltpu.VMEM((rank, LANES), jnp.float32),
             pltpu.VMEM((3 * rank, point_count), jnp.bfloat16),
-            pltpu.VMEM((rank, point_count), jnp.float32),
-            pltpu.VMEM(kept.shape, jnp.float32),
-            pltpu.SemaphoreType.DMA((point_count // (2 * LANES) + 1,)),
         ],
+        compiler_params=pltpu.CompilerParams(vmem_limit_bytes=24 << 20),
         name="factor_columns",
     )(*(pltpu.with_memory_space_constraint(v, pltpu.VMEM) for v in (got, scaled, kept, local)))
+
+
+def store_kernel(factor_ref, resid_ref, factor_out, resid_out, sems):
+    rank = factor_ref.shape[0]
+    count = sems.shape[0] - 1
+    part = rank // count
+    copies = [pltpu.make_async_copy(resid_ref, resid_out, sems.at[count])]
+    for i in range(count):
+        rows = slice(i * part, (i + 1) * part)
+        copies.append(pltpu.make_async_copy(factor_ref.at[rows, :], factor_out.at[rows, :], sems.at[i]))
+    for copy in copies:
+        copy.start()
+    for copy in copies:
+        copy.wait()
+
+
+def store_call(factor, resid):
+    vmem = pl.BlockSpec(memory_space=pltpu.VMEM)
+    hbm = pl.BlockSpec(memory_space=pl.ANY)
+    return pl.pallas_call(
+        store_kernel,
+        out_shape=(jax.ShapeDtypeStruct(factor.shape, factor.dtype), jax.ShapeDtypeStruct(resid.shape, resid.dtype)),
+        in_specs=[vmem] * 2,
+        out_specs=(hbm,) * 2,
+        scratch_shapes=[pltpu.SemaphoreType.DMA((9,))],
+        cost_estimate=pl.CostEstimate(flops=4_000_000_000, bytes_accessed=2 * factor.size * 4, transcendentals=0),
+        compiler_params=pltpu.CompilerParams(vmem_limit_bytes=1 << 20),
+        name="store_factor",
+    )(*(pltpu.with_memory_space_constraint(v, pltpu.VMEM) for v in (factor, resid)))
 
 
 def body(sizes, points, scales, noise_var, pivots):
@@ -320,7 +337,11 @@
     got = exchange(send.reshape(copies, rows, 1, LANES), GATHER, sizes)
     got = got.reshape(-1, LANES)
     factor, resid, sums = factor_call(block_rows, devices * point_count, sum_copies, got, scaled, kept, local)
-    parts = exchange(sums.reshape(sum_copies, 1, LANES), REDUCE, sizes)
+    own = sums[:1]
+    other = lax.ppermute(own, "c", ((0, 1), (1, 0)))
+    factor, resid = store_call(factor, resid)
+    both, factor, resid = lax.optimization_barrier((own + other, factor, resid))
+    parts = exchange(jnp.broadcast_to(both[None], (group_size(REDUCE[1], sizes), 1, LANES)), REDUCE[1:], sizes)
     means = jnp.sum(parts, axis=0)[0, :blocks]
     return factor, resid.reshape(point_count), means
 

time: 58.2 us -> 58 us (level)
  waiting for transfers between devices: 1.05 us -> 0.01 us
  Pallas kernels: 7.1 us -> 7.7 us
    pallas_call x0 -> x1, Pallas kernels: none -> 1.39 us  [store_call(): pl.pallas_call(store_kernel, out_shape=(jax.ShapeDtypeStruct(factor.shape...]
    ppermute x1, waiting for transfers between devices: 1.05 us -> 0.01 us  [body(): other = lax.ppermute(own, 'c', ((0, 1), (1, 0)))]
    pallas_call x1, Pallas kernels: 5.97 us -> 5.18 us  [factor_call(): pl.pallas_call(functools.partial(main_kernel, block_rows, total), out_sha...]
  transfers between devices with their start and end apart: 1 -> 1, of which waited for: 1 -> 0; matrix products, arithmetic and copies ran while one was open for 0% -> 0% of each run, Pallas kernels for 0% -> 2%
where the time goes in v4:
time: 58 us; the launch traced here: 57.8 us
  blocking collectives  48.6 us (84%)
  Pallas kernels  7.7 us (13%)
  between operations  0.68 us (1%)
  local copies, waits for them, and re-layouts  0.6 us (1%)
    all_to_all x3, blocking collectives, exchange(): stacked = lax.all_to_all(stacked, group, 0, 0)  48.6 us
    pallas_call x1, Pallas kernels, factor_call(): pl.pallas_call(functools.partial(main_kernel, block_rows, total), out_sha...  5.18 us
    pallas_call x1, Pallas kernels, store_call(): pl.pallas_call(store_kernel, out_shape=(jax.ShapeDtypeStruct(factor.shape...  1.39 us
  transfers between devices with their start and end apart: 1, of which 0 were waited for; matrix products, arithmetic and copies ran while one was open for 0% of the time, Pallas kernels for 2%

profile of v4, /device:TPU:1, one launch (start us, length us, event | category | flops | bytes accessed | tf_op | source)
XLA Modules:
  0.0 57.8 jit_solution(9376282182580611239)
XLA Ops:
  0.6 1.1 %pick_pivots.1 = (f32[144,128]{1,0:T(8,128)S(1)}, f32[8,4096]{1,0:T(8,128)S(1)}, s32[8,128]{1,0:T(8,128)S(1)}, f32[32,128]{1,0:T(8,128)S(1)}) custom-call(f32[8,4096]{1,0:T(8,128)} %points_ref.1, f32[32,128]{1,0:T(8,128)} %bitcast.12, f32[8]{0:T(128)} %scales_ref.1, s32[8,16]{1,0:T(8,128)} %pivots_ref.1), custom_call_target="tpu_custom_call" | custom-call | tf_op jit(solution)/shard_map/pick_pivots/pallas_call | solution.py:324
  1.8 13.9 %all_to_all.15 = f32[16,9,1,128]{3,2,1,0:T(1,128)S(1)} all-to-all(f32[16,9,1,128]{3,2,1,0:T(1,128)S(1)} %bitcast.10), channel_id=1, replica_groups=mesh['x'=4,'y'=4,'z'=8,'c'=2] {'x','y'}, dimensions={0} | all-to-all | bytes 147456 | tf_op jit(solution)/shard_map/all_to_all | solution.py:254
  15.7 0.1 reduce_sum.20
  15.8 18.3 %all_to_all.16 = f32[16,9,1,128]{3,2,1,0:T(1,128)S(1)} all-to-all(f32[16,9,1,128]{3,2,1,0:T(1,128)S(1)} %broadcast_in_dim.6), channel_id=1, replica_groups=mesh['x'=4,'y'=4,'z'=8,'c'=2] {'z','c'}, dimensions={0} | all-to-all | bytes 147456 | tf_op jit(solution)/shard_map/all_to_all | solution.py:254
  34.1 5.2 %factor_columns.1 = (f32[128,4096]{1,0:T(8,128)S(1)}, f32[32,128]{1,0:T(8,128)S(1)}, f32[2,128]{1,0:T(2,128)S(1)}) custom-call(f32[144,128]{1,0:T(8,128)S(1)} %bitcast.9, f32[8,4096]{1,0:T(8,128)S(1)} %get-tuple-element.16.scaled_ref, f32[32,128]{1,0:T(8,128)S(1)} %get-tuple-element.17.noise_ref, s32[8,128]{1,0:T(8,128)S(1)} %get-tuple-element.18.local_ref), custom_call_target="tpu_custom_call" | custom-call | tf_op jit(solution)/shard_map/factor_columns/pallas_call | solution.py:266
  39.3 0.1 collective-permute-start
  39.4 1.4 %store_factor.1 = (f32[128,4096]{1,0:T(8,128)}, f32[32,128]{1,0:T(8,128)}) custom-call(f32[128,4096]{1,0:T(8,128)S(1)} %get-tuple-element.20.factor_ref, f32[32,128]{1,0:T(8,128)S(1)} %get-tuple-element.21.resid_ref), custom_call_target="tpu_custom_call" | custom-call | flops 4000000000 | bytes 4194304 | tf_op jit(solution)/shard_map/store_factor/pallas_call | solution.py:302
  40.8 0.0 collective-permute-done
  40.9 16.3 %all_to_all.17 = f32[128,1,128]{2,1,0:T(1,128)S(1)} all-to-all(f32[128,1,128]{2,1,0:T(1,128)S(1)} %broadcast_in_dim.16), channel_id=1, replica_groups=mesh['x'=4,'y'=4,'z'=8,'c'=2] {'x','y','z'}, dimensions={0} | all-to-all | bytes 131072 | tf_op jit(solution)/shard_map/all_to_all | solution.py:254
  57.2 0.5 slice_bitcast_fusion
  (5 shorter events, 0.1 us)
Async XLA Ops:
  39.3 1.5 %collective-permute-start = (f32[1,128]{1,0:T(1,128)S(1)}, f32[1,128]{1,0:T(1,128)S(1)}, u32[]{:S(2)}, u32[]{:S(2)}) collective-permute-start(f32[1,128]{1,0:T(1,128)S(1)} %slice.6), channel_id=1, source_target_pairs={{0,1},{1,0},{2,3},{3,2},{4,5},{5,4},{6,7},{7,6},{8,9},{9,8},{10,11... | collective-permute-start | bytes 1544 | tf_op jit(solution)/shard_map/ppermute | solution.py:341

commit v5 on v4

--- a/solution.py
+++ b/solution.py
@@ -10,13 +10,14 @@
 from jax.sharding import PartitionSpec as P
 
 AXES = ("x", "y", "z", "c")
-GATHER = (("x", "y"), ("z", "c"))
-REDUCE = (("c",), ("x", "y", "z"))
+CHIPS = ("x", "y", "z")
+CORES = "c"
 LANES = 128
 SUB = 8
 ROOT = math.sqrt(0.5 * math.log2(math.e))
 HIGH = lax.Precision.HIGHEST
 GRID = 16.0
+SLOTS = 14
 
 
 def iota(shape, dim):
@@ -31,7 +32,7 @@
     return jnp.broadcast_to(tile[:, col : col + 1], tile.shape)
 
 
-def local_pivots(pivots_ref, wide_ref, sizes, point_count):
+def pivot_row(pivots_ref, wide_ref):
     blocks, block_rows = pivots_ref.shape
     wide_ref[...] = jnp.zeros_like(wide_ref)
     wide_ref[:, 0:block_rows] = pivots_ref[...]
@@ -40,41 +41,127 @@
     row = jnp.zeros((SUB, LANES), jnp.int32)
     for block in range(blocks):
         row = jnp.where(lane // block_rows == block, splat_row(spread, block), row)
-    index = lax.axis_index(AXES[0])
-    for axis in AXES[1:]:
-        index = index * sizes[axis] + lax.axis_index(axis)
-    return row - index * point_count
-
-
-def pre_kernel(sizes, copies, points_ref, noise_ref, scales_ref, pivots_ref, send_ref, scaled_ref, local_ref, kept_ref, wide_ref):
+    return row
+
+
+def chip_index(sizes):
+    chip = lax.axis_index(CHIPS[0])
+    for axis in CHIPS[1:]:
+        chip = chip * sizes[axis] + lax.axis_index(axis)
+    return chip
+
+
+def slots_of_lanes(rank, dim):
+    lane = iota((rank, LANES), 1)
+    slot = jnp.where(lane < dim * SLOTS, lane // dim, lane - dim * SLOTS)
+    return jnp.where(slot < SLOTS, slot, -2 - 2 * rank).astype(jnp.float32)
+
+
+def message(coords, noise, holds):
+    dim = coords.shape[0]
+    rank = holds.shape[0]
+    index = jnp.sum(jnp.where(holds, iota((rank, LANES), 0) + 1, 0).astype(jnp.float32), axis=0, keepdims=True).astype(jnp.int32)
+    index = jnp.broadcast_to(index, (SUB, LANES))
+    taken = jnp.maximum(index - 1, 0)
+    lane = iota((SUB, LANES), 1)
+    place = jnp.where(lane < dim * SLOTS, lane % dim, dim)
+    values = jnp.where(iota((SUB, LANES), 0) == place, jnp.take_along_axis(coords, taken, axis=1, mode="promise_in_bounds"), 0.0)
+    row = jnp.sum(values, axis=0, keepdims=True)
+    noises = jnp.take_along_axis(jnp.broadcast_to(noise, (SUB, LANES)), taken, axis=1, mode="promise_in_bounds")
+    row = row + jnp.where(place == dim, noises, 0.0)[:1]
+    return jnp.where(index[:1] > 0, row, 0.0)
+
+
+def pre_kernel(
+    sizes, points_hbm, noise_hbm, scales_hbm, pivots_hbm,
+    send_ref, values_ref, scaled_ref, about_ref, kept_ref, points_ref, scales_ref, pivots_ref, wide_ref, sems,
+):
+    copies = []
+    for i, (source, target) in enumerate(((pivots_hbm, pivots_ref), (points_hbm, points_ref), (noise_hbm, kept_ref), (scales_hbm, scales_ref))):
+        copies.append(pltpu.make_async_copy(source, target, sems.at[i]))
+        copies[i].start()
     dim, point_count = points_ref.shape
     tiles = point_count // LANES
-    local = local_pivots(pivots_ref, wide_ref, sizes, point_count)
-    local_ref[...] = local
     sub = iota((SUB, LANES), 0)
+    lane = iota((SUB, LANES), 1)
+    chip = chip_index(sizes)
+
+    copies[0].wait()
+    pivot = pivot_row(pivots_ref, wide_ref)
+    rank = pivots_ref.shape[0] * pivots_ref.shape[1]
+    local = pivot - (chip * sizes[CORES] + lax.axis_index(CORES)) * point_count
+    owner = pivot // (point_count * sizes[CORES])
+    owner_row = jnp.broadcast_to(owner[:1].astype(jnp.float32), (rank, LANES))
+    owner_col = jnp.transpose(owner_row)
+    same = owner_col == owner_row
+    first, second = iota((rank, LANES), 0), iota((rank, LANES), 1)
+    place_row = jnp.sum(jnp.where(same & (first < second), 1.0, 0.0), axis=0, keepdims=True)
+    place_col = jnp.sum(jnp.where(same & (second < first), 1.0, 0.0), axis=1, keepdims=True)
+    place = jnp.broadcast_to(place_row, (SUB, LANES))
+    more = jnp.broadcast_to(jnp.max(place, axis=1, keepdims=True), (SUB, LANES)).astype(jnp.int32) // SLOTS
+    about_ref[...] = jnp.where(sub == 0, local, jnp.where(sub == 1, owner, jnp.where(sub == 2, place.astype(jnp.int32), more)))
+    mine = jnp.where(owner_col == chip.astype(jnp.float32), jnp.broadcast_to(place_col, (rank, LANES)), -1.0 - rank)
+    holds = mine == slots_of_lanes(rank, dim)
+
+    owned = (local >= 0) & (local < point_count)
+    position = jnp.where(owned, local, -1)
+    tile_of = position >> 7
+    lane_of = position & (LANES - 1)
+    for copy in copies[1:]:
+        copy.wait()
     scale = jnp.zeros((SUB, LANES), jnp.float32)
     for d in range(dim):
         scale = jnp.where(sub == d, scales_ref[d], scale)
     factor = ROOT / scale
-    owned = (local >= 0) & (local < point_count)
-    position = jnp.where(owned, local, -1)
-    tile_of = position >> 7
-    lane_of = position & (LANES - 1)
     coords = jnp.zeros((SUB, LANES), jnp.float32)
     for t in range(tiles):
         tile = points_ref[:, t * LANES : (t + 1) * LANES] * factor
         scaled_ref[:, t * LANES : (t + 1) * LANES] = tile
         found = jnp.take_along_axis(tile, lane_of, axis=1, mode="promise_in_bounds")
         coords = jnp.where(tile_of == t, found, coords)
-    kept_ref[...] = noise_ref[...]
     noise = jnp.zeros((SUB, LANES), jnp.float32)
     for a in range(tiles // SUB):
-        found = jnp.take_along_axis(noise_ref[a * SUB : (a + 1) * SUB, :], lane_of, axis=1, mode="promise_in_bounds")
+        found = jnp.take_along_axis(kept_ref[a * SUB : (a + 1) * SUB, :], lane_of, axis=1, mode="promise_in_bounds")
         noise = noise + jnp.where(tile_of == sub + a * SUB, found, 0.0)
     noise = jnp.sum(noise, axis=0, keepdims=True)
-    for i in range(copies):
-        send_ref[i * (dim + 1) : i * (dim + 1) + dim, :] = coords
-        send_ref[i * (dim + 1) + dim : (i + 1) * (dim + 1), :] = noise
+    values_ref[0:dim, :] = coords
+    values_ref[dim:, :] = jnp.broadcast_to(noise, (SUB, LANES))
+    send_ref[...] = message(coords, noise, holds)
+
+
+def pack_kernel(sizes, number_ref, values_ref, about_ref, send_ref):
+    dim = SUB
+    rank = about_ref.shape[1]
+    owner = jnp.transpose(jnp.broadcast_to(about_ref[1:2, :], (rank, LANES)).astype(jnp.float32))
+    place = jnp.transpose(jnp.broadcast_to(about_ref[2:3, :], (rank, LANES)).astype(jnp.float32))
+    first = (number_ref[0] * SLOTS).astype(jnp.float32)
+    mine = jnp.where(owner == chip_index(sizes).astype(jnp.float32), place - first, -1.0 - rank)
+    send_ref[...] = message(values_ref[0:dim, :], values_ref[dim : dim + 1, :], mine == slots_of_lanes(rank, dim))
+
+
+def unpack(got, about_ref, number, dim):
+    rank = about_ref.shape[1]
+    chips = got.shape[0]
+    owner = jnp.broadcast_to(about_ref[1:2, :], (chips, rank))
+    slot = jnp.broadcast_to(about_ref[2:3, :], (SUB, rank)) - number * SLOTS
+    pick = jnp.where(owner == iota((chips, rank), 0), 1.0, 0.0).astype(jnp.bfloat16)
+    turned = jnp.concatenate(pieces(jnp.transpose(got)), axis=1)
+    picked = jnp.dot(turned, jnp.concatenate([pick] * 3, axis=0), preferred_element_type=jnp.float32)
+    coords = jnp.zeros((dim, rank), jnp.float32)
+    for s in range(SLOTS):
+        coords = jnp.where(slot == s, picked[s * dim : (s + 1) * dim, :], coords)
+    noise = jnp.zeros((SUB, rank), jnp.float32)
+    sub = iota((SUB, rank), 0)
+    for at in range(dim * SLOTS, LANES, SUB):
+        noise = noise + jnp.where((slot == sub + (at - dim * SLOTS)) & (slot < SLOTS), picked[at : at + SUB, :], 0.0)
+    return coords, jnp.sum(noise, axis=0, keepdims=True)
+
+
+def unpack_kernel(number_ref, got_ref, about_ref, before_ref, after_ref):
+    dim = SUB
+    coords, noise = unpack(got_ref[...], about_ref, number_ref[0], dim)
+    after_ref[0:dim, :] = before_ref[0:dim, :] + coords
+    after_ref[dim:, :] = before_ref[dim:, :] + noise
 
 
 def pieces(value):
@@ -128,25 +215,22 @@
 
 
 def main_kernel(
-    block_rows, total, got_ref, scaled_ref, noise_ref, local_ref,
+    block_rows, total, got_ref, extra_ref, scaled_ref, noise_ref, about_ref,
     out_ref, resid_ref, sums_ref, side_ref, pair_ref, cov_ref,
 ):
     dim, point_count = scaled_ref.shape
     rank = pair_ref.shape[0]
     blocks = rank // block_rows
     halves = block_rows // SUB
-    rows = dim + 1
     tiles_n = point_count // LANES
     width = 2 * LANES
     sub = iota((SUB, LANES), 0)
     lane = iota((SUB, LANES), 1)
 
-    coords = got_ref[0:dim, :]
-    noise_p = got_ref[dim:rows, :]
-    for i in range(1, got_ref.shape[0] // rows):
-        coords = coords + got_ref[i * rows : i * rows + dim, :]
-        noise_p = noise_p + got_ref[i * rows + dim : (i + 1) * rows, :]
-    local = local_ref[...].astype(jnp.float32)
+    coords, noise_p = unpack(got_ref[...], about_ref, 0, dim)
+    coords = coords + extra_ref[0:dim, :]
+    noise_p = noise_p + extra_ref[dim : dim + 1, :]
+    local = jnp.broadcast_to(about_ref[0:1, :], (SUB, LANES)).astype(jnp.float32)
     wanted = jnp.broadcast_to(jnp.transpose(local)[:, :1], (rank, LANES))
     pivot_side = jnp.transpose(jnp.concatenate(features(coords, False), axis=0)).astype(jnp.bfloat16)
     own_side = jnp.concatenate(features(coords, True), axis=0).astype(jnp.bfloat16)
@@ -242,35 +326,18 @@
     sums_ref[...] = jnp.broadcast_to(jnp.sum(jnp.where(sub == lane, means, 0.0), axis=0, keepdims=True), sums_ref.shape)
 
 
-def exchange(stacked, groups, sizes):
-    for i, group in enumerate(groups):
-        if i > 0:
-            value = jnp.sum(stacked, axis=0)
-            stacked = jnp.broadcast_to(value[None], (group_size(group, sizes),) + value.shape)
-        if group == ("c",):
-            other = lax.ppermute(stacked[0], "c", ((0, 1), (1, 0)))
-            stacked = jnp.stack([stacked[0], other])
-        else:
-            stacked = lax.all_to_all(stacked, group, 0, 0)
-    return stacked
-
-
-def group_size(group, sizes):
-    return math.prod(sizes[axis] for axis in group)
-
-
-def factor_call(block_rows, total, sum_copies, got, scaled, kept, local):
-    point_count = scaled.shape[1]
-    rank = local.shape[1]
+def factor_call(block_rows, total, *operands):
+    point_count = operands[2].shape[1]
+    rank = operands[4].shape[1]
     vmem = pl.BlockSpec(memory_space=pltpu.VMEM)
     return pl.pallas_call(
         functools.partial(main_kernel, block_rows, total),
         out_shape=(
             pltpu.VMEM((rank, point_count), jnp.float32),
-            pltpu.VMEM(kept.shape, jnp.float32),
-            pltpu.VMEM((sum_copies, LANES), jnp.float32),
+            pltpu.VMEM((point_count // LANES, LANES), jnp.float32),
+            pltpu.VMEM((1, LANES), jnp.float32),
         ),
-        in_specs=[vmem] * 4,
+        in_specs=[vmem] * 5,
         out_specs=(vmem,) * 3,
         scratch_shapes=[
             pltpu.VMEM((12 * SUB, point_count), jnp.bfloat16),
@@ -279,7 +346,11 @@
         ],
         compiler_params=pltpu.CompilerParams(vmem_limit_bytes=24 << 20),
         name="factor_columns",
-    )(*(pltpu.with_memory_space_constraint(v, pltpu.VMEM) for v in (got, scaled, kept, local)))
+    )(*in_vmem(*operands))
+
+
+def in_vmem(*values):
+    return [pltpu.with_memory_space_constraint(value, pltpu.VMEM) for value in values]
 
 
 def store_kernel(factor_ref, resid_ref, factor_out, resid_out, sems):
@@ -308,41 +379,78 @@
         cost_estimate=pl.CostEstimate(flops=4_000_000_000, bytes_accessed=2 * factor.size * 4, transcendentals=0),
         compiler_params=pltpu.CompilerParams(vmem_limit_bytes=1 << 20),
         name="store_factor",
-    )(*(pltpu.with_memory_space_constraint(v, pltpu.VMEM) for v in (factor, resid)))
+    )(*in_vmem(factor, resid))
+
+
+def to_chips(row, sizes):
+    chips = math.prod(sizes[axis] for axis in CHIPS)
+    return lax.all_to_all(jnp.broadcast_to(row[None], (chips,) + row.shape), CHIPS, 0, 0)
+
+
+def of_chip(row):
+    return row + lax.ppermute(row, CORES, ((0, 1), (1, 0)))
 
 
 def body(sizes, points, scales, noise_var, pivots):
     dim, point_count = points.shape
     blocks, block_rows = pivots.shape
     devices = math.prod(sizes.values())
-    rows = dim + 1
-    copies = group_size(GATHER[0], sizes)
-    sum_copies = group_size(REDUCE[0], sizes)
+    chips = devices // sizes[CORES]
     noise = noise_var.reshape(point_count // LANES, LANES)
     vmem = pl.BlockSpec(memory_space=pltpu.VMEM)
     smem = pl.BlockSpec(memory_space=pltpu.SMEM)
-    send, scaled, local, kept = pl.pallas_call(
-        functools.partial(pre_kernel, sizes, copies),
+    hbm = pl.BlockSpec(memory_space=pl.ANY)
+    send, values, scaled, about, kept = pl.pallas_call(
+        functools.partial(pre_kernel, sizes),
         out_shape=(
-            pltpu.VMEM((copies * rows, LANES), jnp.float32),
+            pltpu.VMEM((1, LANES), jnp.float32),
+            pltpu.VMEM((2 * SUB, LANES), jnp.float32),
             pltpu.VMEM((dim, point_count), jnp.float32),
             pltpu.VMEM((SUB, LANES), jnp.int32),
             pltpu.VMEM(noise.shape, jnp.float32),
         ),
-        in_specs=[vmem, vmem, smem, vmem],
-        out_specs=(vmem,) * 4,
-        scratch_shapes=[pltpu.VMEM((SUB, LANES), jnp.int32)],
+        in_specs=[hbm] * 4,
+        out_specs=(vmem,) * 5,
+        scratch_shapes=[
+            pltpu.VMEM((dim, point_count), jnp.float32),
+            pltpu.SMEM((dim,), jnp.float32),
+            pltpu.VMEM((blocks, block_rows), jnp.int32),
+            pltpu.VMEM((SUB, LANES), jnp.int32),
+            pltpu.SemaphoreType.DMA((4,)),
+        ],
         name="pick_pivots",
     )(points, noise, scales, pivots)
-    got = exchange(send.reshape(copies, rows, 1, LANES), GATHER, sizes)
-    got = got.reshape(-1, LANES)
-    factor, resid, sums = factor_call(block_rows, devices * point_count, sum_copies, got, scaled, kept, local)
-    own = sums[:1]
-    other = lax.ppermute(own, "c", ((0, 1), (1, 0)))
+    row = of_chip(send)
+    last, row = lax.optimization_barrier((about[3, 0], row))
+    got = to_chips(row, sizes).reshape(chips, LANES)
+
+    def another(state):
+        number, end, extra = state
+        packed = pl.pallas_call(
+            functools.partial(pack_kernel, sizes),
+            out_shape=jax.ShapeDtypeStruct((1, LANES), jnp.float32),
+            in_specs=[smem] + [vmem] * 2,
+            out_specs=vmem,
+            name="pack_more",
+        )(number[None], values, about)
+        more_got = to_chips(of_chip(packed), sizes).reshape(chips, LANES)
+        extra = pl.pallas_call(
+            unpack_kernel,
+            out_shape=jax.ShapeDtypeStruct(extra.shape, jnp.float32),
+            in_specs=[smem] + [vmem] * 3,
+            out_specs=vmem,
+            name="unpack_more",
+        )(number[None], more_got, about, extra)
+        return number + 1, end, extra
+
+    start = (jnp.int32(1), last, jnp.zeros((2 * SUB, LANES), jnp.float32))
+    extra = lax.while_loop(lambda state: state[0] <= state[1], another, start)[2]
+
+    factor, resid, sums = factor_call(block_rows, devices * point_count, got, extra, scaled, kept, about)
+    both = of_chip(sums)
     factor, resid = store_call(factor, resid)
-    both, factor, resid = lax.optimization_barrier((own + other, factor, resid))
-    parts = exchange(jnp.broadcast_to(both[None], (group_size(REDUCE[1], sizes), 1, LANES)), REDUCE[1:], sizes)
-    means = jnp.sum(parts, axis=0)[0, :blocks]
+    both, factor, resid = lax.optimization_barrier((both, factor, resid))
+    means = jnp.sum(to_chips(both, sizes), axis=0)[0, :blocks]
     return factor, resid.reshape(point_count), means
 
 

time: 58 us -> 56.4 us (0.972)
  blocking collectives: 48.6 us -> 40.4 us
  starting transfers between devices: 0.13 us -> 5.07 us
    all_to_all x3 -> x2, blocking collectives: 48.6 us -> 40.4 us  [to_chips(): lax.all_to_all(jnp.broadcast_to(row[None], (chips,) + row.shape), CHIPS,...]
    ppermute x1 -> x2, starting transfers between devices: 0.13 us -> 5.07 us  [of_chip(): return row + lax.ppermute(row, CORES, ((0, 1), (1, 0)))]
  transfers between devices with their start and end apart: 1 -> 2, of which waited for: 0 -> 1; matrix products, arithmetic and copies ran while one was open for 0% -> 1% of each run, Pallas kernels for 2% -> 2%
where the time goes in v5:
time: 56.4 us; the launch traced here: 56.1 us
  blocking collectives  40.4 us (72%)
  Pallas kernels  7.97 us (14%)
  starting transfers between devices  5.07 us (9%)
  local copies, waits for them, and re-layouts  1.09 us (2%)
  between operations  0.69 us (1%)
    all_to_all x2, blocking collectives, to_chips(): lax.all_to_all(jnp.broadcast_to(row[None], (chips,) + row.shape), CHIPS,...  40.4 us
    pallas_call x1, Pallas kernels, factor_call(): pl.pallas_call(functools.partial(main_kernel, block_rows, total), out_sha...  5.37 us
    ppermute x2, starting transfers between devices, of_chip(): return row + lax.ppermute(row, CORES, ((0, 1), (1, 0)))  5.07 us
    pallas_call x1, Pallas kernels, store_call(): pl.pallas_call(store_kernel, out_shape=(jax.ShapeDtypeStruct(factor.shape...  1.39 us
    pallas_call x1, Pallas kernels, body(): pl.pallas_call(functools.partial(pre_kernel, sizes), out_shape=(pltpu.VME...  1.22 us
  transfers between devices with their start and end apart: 2, of which 1 were waited for; matrix products, arithmetic and copies ran while one was open for 1% of the time, Pallas kernels for 2%

profile of v5, /device:TPU:1, one launch (start us, length us, event | category | flops | bytes accessed | tf_op | source)
XLA Modules:
  0.0 56.1 jit_solution(4888364841695431553)
XLA Ops:
  0.6 1.2 %pick_pivots.1 = (f32[1,128]{1,0:T(1,128)S(1)}, f32[16,128]{1,0:T(8,128)S(1)}, f32[8,4096]{1,0:T(8,128)S(1)}, s32[8,128]{1,0:T(8,128)S(1)}, f32[32,128]{1,0:T(8,128)S(1)}) custom-call(f32[8,4096]{1,0:T(8,128)} %points_hbm.1, f32[32,128]{1,0:T(8,128)} %bitcast.23, f32[8]{0:T(128)} %scales_hbm.1, s32[8,16]{1,0:T(8,128)} %pivots_hbm.1), custom_call_target="tpu_custom_call" | custom-call | tf_op jit(solution)/shard_map/pick_pivots/pallas_call | solution.py:403
  1.9 3.3 %collective-permute-start.1 = (f32[1,128]{1,0:T(1,128)S(1)}, f32[1,128]{1,0:T(1,128)S(1)}, u32[]{:S(2)}, u32[]{:S(2)}) collective-permute-start(f32[1,128]{1,0:T(1,128)S(1)} %get-tuple-element.47), channel_id=1, source_target_pairs={{0,1},{1,0},{2,3},{3,2},{4,5},{5,4},{6,7},{7,6},{8,9},{9,8},{10,11... | collective-permute-start | bytes 1544 | tf_op jit(solution)/shard_map/ppermute | solution.py:391
  5.1 0.5 slice.6
  5.7 0.3 collective-permute-done.1
  6.0 0.6 %while.10 = (s32[]{:T(128)}, f32[16,128]{1,0:T(8,128)S(1)}, s32[]{:T(128)}, f32[16,128]{1,0:T(8,128)S(1)}, s32[8,128]{1,0:T(8,128)S(1)}, /*index=5*/s32[]{:T(128)}) while((s32[]{:T(128)}, f32[16,128]{1,0:T(8,128)S(1)}, s32[]{:T(128)}, f32[16,128]{1,0:T(8,128)S(1)}, s32[8,128]{1,0:T(8,128)S(1)}, /*index=5*/s32[]{:T(128)}) %tuple.26), condition=%wide.region_1.0_spmd, body=%wide.region_0.0_spmd.sunk | while | flops 130 | bytes 544945 | solution.py:447
  6.6 24.2 %all_to_all.16 = f32[128,1,128]{2,1,0:T(1,128)S(1)} all-to-all(f32[128,1,128]{2,1,0:T(1,128)S(1)} %broadcast_in_dim.32), channel_id=1, replica_groups=mesh['x'=4,'y'=4,'z'=8,'c'=2] {'x','y','z'}, dimensions={0} | all-to-all | bytes 131072 | tf_op jit(solution)/shard_map/all_to_all | solution.py:387
  30.8 5.4 %factor_columns.1 = (f32[128,4096]{1,0:T(8,128)S(1)}, f32[32,128]{1,0:T(8,128)S(1)}, f32[1,128]{1,0:T(1,128)S(1)}) custom-call(f32[128,128]{1,0:T(8,128)S(1)} %bitcast.20, f32[16,128]{1,0:T(8,128)S(1)} %get-tuple-element.51.extra_ref, f32[8,4096]{1,0:T(8,128)S(1)} %get-tuple-element.52.scaled_ref, f32[32,128]{1,0:T(8,128)S(1)} %get-tuple-element.53.noise_ref, ...), custom_call_target="tpu_custom_call" | custom-call | tf_op jit(solution)/shard_map/factor_columns/pallas_call | solution.py:333
  36.1 1.8 %collective-permute-start.2 = (f32[1,128]{1,0:T(1,128)S(1)}, f32[1,128]{1,0:T(1,128)S(1)}, u32[]{:S(2)}, u32[]{:S(2)}) collective-permute-start(f32[1,128]{1,0:T(1,128)S(1)} %get-tuple-element.54), channel_id=1, source_target_pairs={{0,1},{1,0},{2,3},{3,2},{4,5},{5,4},{6,7},{7,6},{8,9},{9,8},{10,11... | collective-permute-start | bytes 1544 | tf_op jit(solution)/shard_map/ppermute | solution.py:391
  37.9 1.4 %store_factor.1 = (f32[128,4096]{1,0:T(8,128)}, f32[32,128]{1,0:T(8,128)}) custom-call(f32[128,4096]{1,0:T(8,128)S(1)} %get-tuple-element.55.factor_ref, f32[32,128]{1,0:T(8,128)S(1)} %get-tuple-element.56.resid_ref), custom_call_target="tpu_custom_call" | custom-call | flops 4000000000 | bytes 4194304 | tf_op jit(solution)/shard_map/store_factor/pallas_call | solution.py:373
  39.3 0.0 collective-permute-done.2
  39.4 16.2 %all_to_all.17 = f32[128,1,128]{2,1,0:T(1,128)S(1)} all-to-all(f32[128,1,128]{2,1,0:T(1,128)S(1)} %broadcast_in_dim.35), channel_id=1, replica_groups=mesh['x'=4,'y'=4,'z'=8,'c'=2] {'x','y','z'}, dimensions={0} | all-to-all | bytes 131072 | tf_op jit(solution)/shard_map/all_to_all | solution.py:387
  55.6 0.5 slice_bitcast_fusion
  (6 shorter events, 0.1 us)
Async XLA Ops:
  1.9 4.1 %collective-permute-start.1 = (f32[1,128]{1,0:T(1,128)S(1)}, f32[1,128]{1,0:T(1,128)S(1)}, u32[]{:S(2)}, u32[]{:S(2)}) collective-permute-start(f32[1,128]{1,0:T(1,128)S(1)} %get-tuple-element.47), channel_id=1, source_target_pairs={{0,1},{1,0},{2,3},{3,2},{4,5},{5,4},{6,7},{7,6},{8,9},{9,8},{10,11... | collective-permute-start | bytes 1544 | tf_op jit(solution)/shard_map/ppermute | solution.py:391
  36.1 3.2 %collective-permute-start.2 = (f32[1,128]{1,0:T(1,128)S(1)}, f32[1,128]{1,0:T(1,128)S(1)}, u32[]{:S(2)}, u32[]{:S(2)}) collective-permute-start(f32[1,128]{1,0:T(1,128)S(1)} %get-tuple-element.54), channel_id=1, source_target_pairs={{0,1},{1,0},{2,3},{3,2},{4,5},{5,4},{6,7},{7,6},{8,9},{9,8},{10,11... | collective-permute-start | bytes 1544 | tf_op jit(solution)/shard_map/ppermute | solution.py:391

commit v6 on v5

--- a/solution.py
+++ b/solution.py
@@ -9,13 +9,13 @@
 from jax.sharding import Mesh
 from jax.sharding import PartitionSpec as P
 
+
 AXES = ("x", "y", "z", "c")
 CHIPS = ("x", "y", "z")
 CORES = "c"
 LANES = 128
 SUB = 8
 ROOT = math.sqrt(0.5 * math.log2(math.e))
-HIGH = lax.Precision.HIGHEST
 GRID = 16.0
 SLOTS = 14
 
@@ -172,7 +172,7 @@
 
 
 def features(coords, second):
-    dim, count = coords.shape
+    _, count = coords.shape
     sub = iota((SUB, count), 0)
     coarse = jnp.round(coords * GRID)
     near = coarse * (1.0 / GRID)
@@ -210,8 +210,7 @@
 
 
 def exponent(left, right):
-    coarse = jnp.dot(left[:, : 2 * SUB], right[: 2 * SUB, :], preferred_element_type=jnp.float32)
-    return coarse + jnp.dot(left[:, 2 * SUB :], right[2 * SUB :, :], preferred_element_type=jnp.float32)
+    return jnp.dot(left, right, preferred_element_type=jnp.float32)
 
 
 def main_kernel(
@@ -421,7 +420,7 @@
         name="pick_pivots",
     )(points, noise, scales, pivots)
     row = of_chip(send)
-    last, row = lax.optimization_barrier((about[3, 0], row))
+    last = lax.optimization_barrier(about[3, 0])
     got = to_chips(row, sizes).reshape(chips, LANES)
 
     def another(state):

time: 56.4 us -> 56.3 us (level)
  no operation moved by 1% of the time
where the time goes in v6:
time: 56.3 us; the launch traced here: 56.1 us
  blocking collectives  40.4 us (72%)
  Pallas kernels  7.96 us (14%)
  starting transfers between devices  5.07 us (9%)
  local copies, waits for them, and re-layouts  1.09 us (2%)
  between operations  0.69 us (1%)
    all_to_all x2, blocking collectives, to_chips(): lax.all_to_all(jnp.broadcast_to(row[None], (chips,) + row.shape), CHIPS,...  40.4 us
    pallas_call x1, Pallas kernels, factor_call(): pl.pallas_call(functools.partial(main_kernel, block_rows, total), out_sha...  5.36 us
    ppermute x2, starting transfers between devices, of_chip(): return row + lax.ppermute(row, CORES, ((0, 1), (1, 0)))  5.07 us
    pallas_call x1, Pallas kernels, store_call(): pl.pallas_call(store_kernel, out_shape=(jax.ShapeDtypeStruct(factor.shape...  1.39 us
    pallas_call x1, Pallas kernels, body(): pl.pallas_call(functools.partial(pre_kernel, sizes), out_shape=(pltpu.VME...  1.22 us
  transfers between devices with their start and end apart: 2, of which 1 were waited for; matrix products, arithmetic and copies ran while one was open for 1% of the time, Pallas kernels for 2%

profile of v6, /device:TPU:1, one launch (start us, length us, event | category | flops | bytes accessed | tf_op | source)
XLA Modules:
  0.0 56.1 jit_solution(2509814579291913059)
XLA Ops:
  0.6 1.2 %pick_pivots.1 = (f32[1,128]{1,0:T(1,128)S(1)}, f32[16,128]{1,0:T(8,128)S(1)}, f32[8,4096]{1,0:T(8,128)S(1)}, s32[8,128]{1,0:T(8,128)S(1)}, f32[32,128]{1,0:T(8,128)S(1)}) custom-call(f32[8,4096]{1,0:T(8,128)} %points_hbm.1, f32[32,128]{1,0:T(8,128)} %bitcast.24, f32[8]{0:T(128)} %scales_hbm.1, s32[8,16]{1,0:T(8,128)} %pivots_hbm.1), custom_call_target="tpu_custom_call" | custom-call | tf_op jit(solution)/shard_map/pick_pivots/pallas_call | solution.py:402
  1.9 3.3 %collective-permute-start.1 = (f32[1,128]{1,0:T(1,128)S(1)}, f32[1,128]{1,0:T(1,128)S(1)}, u32[]{:S(2)}, u32[]{:S(2)}) collective-permute-start(f32[1,128]{1,0:T(1,128)S(1)} %get-tuple-element.44), channel_id=1, source_target_pairs={{0,1},{1,0},{2,3},{3,2},{4,5},{5,4},{6,7},{7,6},{8,9},{9,8},{10,11... | collective-permute-start | bytes 1544 | tf_op jit(solution)/shard_map/ppermute | solution.py:390
  5.1 0.5 slice.6
  5.7 0.3 collective-permute-done.1
  6.0 0.6 %while.10 = (s32[]{:T(128)}, f32[16,128]{1,0:T(8,128)S(1)}, s32[]{:T(128)}, f32[16,128]{1,0:T(8,128)S(1)}, s32[8,128]{1,0:T(8,128)S(1)}, /*index=5*/s32[]{:T(128)}) while((s32[]{:T(128)}, f32[16,128]{1,0:T(8,128)S(1)}, s32[]{:T(128)}, f32[16,128]{1,0:T(8,128)S(1)}, s32[8,128]{1,0:T(8,128)S(1)}, /*index=5*/s32[]{:T(128)}) %tuple.24), condition=%wide.region_1.0_spmd, body=%wide.region_0.0_spmd.sunk | while | flops 130 | bytes 544945 | solution.py:446
  6.6 24.2 %all_to_all.16 = f32[128,1,128]{2,1,0:T(1,128)S(1)} all-to-all(f32[128,1,128]{2,1,0:T(1,128)S(1)} %broadcast_in_dim.32), channel_id=1, replica_groups=mesh['x'=4,'y'=4,'z'=8,'c'=2] {'x','y','z'}, dimensions={0} | all-to-all | bytes 131072 | tf_op jit(solution)/shard_map/all_to_all | solution.py:386
  30.8 5.4 %factor_columns.1 = (f32[128,4096]{1,0:T(8,128)S(1)}, f32[32,128]{1,0:T(8,128)S(1)}, f32[1,128]{1,0:T(1,128)S(1)}) custom-call(f32[128,128]{1,0:T(8,128)S(1)} %bitcast.21, f32[16,128]{1,0:T(8,128)S(1)} %get-tuple-element.47.extra_ref, f32[8,4096]{1,0:T(8,128)S(1)} %get-tuple-element.48.scaled_ref, f32[32,128]{1,0:T(8,128)S(1)} %get-tuple-element.49.noise_ref, ...), custom_call_target="tpu_custom_call" | custom-call | tf_op jit(solution)/shard_map/factor_columns/pallas_call | solution.py:332
  36.1 1.8 %collective-permute-start.2 = (f32[1,128]{1,0:T(1,128)S(1)}, f32[1,128]{1,0:T(1,128)S(1)}, u32[]{:S(2)}, u32[]{:S(2)}) collective-permute-start(f32[1,128]{1,0:T(1,128)S(1)} %get-tuple-element.50), channel_id=1, source_target_pairs={{0,1},{1,0},{2,3},{3,2},{4,5},{5,4},{6,7},{7,6},{8,9},{9,8},{10,11... | collective-permute-start | bytes 1544 | tf_op jit(solution)/shard_map/ppermute | solution.py:390
  37.9 1.4 %store_factor.1 = (f32[128,4096]{1,0:T(8,128)}, f32[32,128]{1,0:T(8,128)}) custom-call(f32[128,4096]{1,0:T(8,128)S(1)} %get-tuple-element.51.factor_ref, f32[32,128]{1,0:T(8,128)S(1)} %get-tuple-element.52.resid_ref), custom_call_target="tpu_custom_call" | custom-call | flops 4000000000 | bytes 4194304 | tf_op jit(solution)/shard_map/store_factor/pallas_call | solution.py:372
  39.3 0.0 collective-permute-done.2
  39.4 16.2 %all_to_all.17 = f32[128,1,128]{2,1,0:T(1,128)S(1)} all-to-all(f32[128,1,128]{2,1,0:T(1,128)S(1)} %broadcast_in_dim.35), channel_id=1, replica_groups=mesh['x'=4,'y'=4,'z'=8,'c'=2] {'x','y','z'}, dimensions={0} | all-to-all | bytes 131072 | tf_op jit(solution)/shard_map/all_to_all | solution.py:386
  55.6 0.5 slice_bitcast_fusion
  (6 shorter events, 0.1 us)
Async XLA Ops:
  1.9 4.1 %collective-permute-start.1 = (f32[1,128]{1,0:T(1,128)S(1)}, f32[1,128]{1,0:T(1,128)S(1)}, u32[]{:S(2)}, u32[]{:S(2)}) collective-permute-start(f32[1,128]{1,0:T(1,128)S(1)} %get-tuple-element.44), channel_id=1, source_target_pairs={{0,1},{1,0},{2,3},{3,2},{4,5},{5,4},{6,7},{7,6},{8,9},{9,8},{10,11... | collective-permute-start | bytes 1544 | tf_op jit(solution)/shard_map/ppermute | solution.py:390
  36.1 3.2 %collective-permute-start.2 = (f32[1,128]{1,0:T(1,128)S(1)}, f32[1,128]{1,0:T(1,128)S(1)}, u32[]{:S(2)}, u32[]{:S(2)}) collective-permute-start(f32[1,128]{1,0:T(1,128)S(1)} %get-tuple-element.50), channel_id=1, source_target_pairs={{0,1},{1,0},{2,3},{3,2},{4,5},{5,4},{6,7},{7,6},{8,9},{9,8},{10,11... | collective-permute-start | bytes 1544 | tf_op jit(solution)/shard_map/ppermute | solution.py:390

commit v7 on v6

--- a/solution.py
+++ b/solution.py
@@ -222,7 +222,7 @@
     blocks = rank // block_rows
     halves = block_rows // SUB
     tiles_n = point_count // LANES
-    width = 2 * LANES
+    width = 4 * LANES
     sub = iota((SUB, LANES), 0)
     lane = iota((SUB, LANES), 1)
 
@@ -293,12 +293,15 @@
     inverse = jnp.where(iota((rank, LANES), 1) <= iota((rank, LANES), 0), pair_ref[...], 0.0)
 
     high, middle, low = pieces(inverse)
-    left = jnp.concatenate([high, high, middle, middle, low, high], axis=1)
+    stacked = jnp.concatenate([jnp.concatenate([high, high], axis=1), jnp.concatenate([middle, middle], axis=1)], axis=0)
+    last = jnp.concatenate([low, high], axis=1)
     block_sums = [jnp.zeros((SUB, LANES), jnp.float32) for _ in range(blocks)]
+    width = 8 * LANES
     for t in range(point_count // width):
         cols_t = slice(t * width, (t + 1) * width)
         large, small = cov_ref[: 2 * rank, cols_t], cov_ref[rank:, cols_t]
-        new = jnp.dot(left, jnp.concatenate([large, large, small], axis=0), preferred_element_type=jnp.float32)
+        both = jnp.dot(stacked, large, preferred_element_type=jnp.float32)
+        new = (both[rank:, :] + jnp.dot(last, small, preferred_element_type=jnp.float32)) + both[:rank, :]
         out_ref[:, cols_t] = new
         for u in range(width // LANES):
             explained = None

time: 56.3 us -> 56.2 us (level)
  no operation moved by 1% of the time
where the time goes in v7:
time: 56.2 us; the launch traced here: 56 us
  blocking collectives  40.4 us (72%)
  Pallas kernels  7.85 us (14%)
  starting transfers between devices  5.07 us (9%)
  local copies, waits for them, and re-layouts  1.09 us (2%)
  between operations  0.69 us (1%)
    all_to_all x2, blocking collectives, to_chips(): lax.all_to_all(jnp.broadcast_to(row[None], (chips,) + row.shape), CHIPS,...  40.4 us
    pallas_call x1, Pallas kernels, factor_call(): pl.pallas_call(functools.partial(main_kernel, block_rows, total), out_sha...  5.25 us
    ppermute x2, starting transfers between devices, of_chip(): return row + lax.ppermute(row, CORES, ((0, 1), (1, 0)))  5.07 us
    pallas_call x1, Pallas kernels, store_call(): pl.pallas_call(store_kernel, out_shape=(jax.ShapeDtypeStruct(factor.shape...  1.39 us
    pallas_call x1, Pallas kernels, body(): pl.pallas_call(functools.partial(pre_kernel, sizes), out_shape=(pltpu.VME...  1.22 us
  transfers between devices with their start and end apart: 2, of which 1 were waited for; matrix products, arithmetic and copies ran while one was open for 1% of the time, Pallas kernels for 2%

profile of v7, /device:TPU:1, one launch (start us, length us, event | category | flops | bytes accessed | tf_op | source)
XLA Modules:
  0.0 56.0 jit_solution(15751145532218128783)
XLA Ops:
  0.6 1.2 %pick_pivots.1 = (f32[1,128]{1,0:T(1,128)S(1)}, f32[16,128]{1,0:T(8,128)S(1)}, f32[8,4096]{1,0:T(8,128)S(1)}, s32[8,128]{1,0:T(8,128)S(1)}, f32[32,128]{1,0:T(8,128)S(1)}) custom-call(f32[8,4096]{1,0:T(8,128)} %points_hbm.1, f32[32,128]{1,0:T(8,128)} %bitcast.24, f32[8]{0:T(128)} %scales_hbm.1, s32[8,16]{1,0:T(8,128)} %pivots_hbm.1), custom_call_target="tpu_custom_call" | custom-call | tf_op jit(solution)/shard_map/pick_pivots/pallas_call | solution.py:405
  1.9 3.3 %collective-permute-start.1 = (f32[1,128]{1,0:T(1,128)S(1)}, f32[1,128]{1,0:T(1,128)S(1)}, u32[]{:S(2)}, u32[]{:S(2)}) collective-permute-start(f32[1,128]{1,0:T(1,128)S(1)} %get-tuple-element.44), channel_id=1, source_target_pairs={{0,1},{1,0},{2,3},{3,2},{4,5},{5,4},{6,7},{7,6},{8,9},{9,8},{10,11... | collective-permute-start | bytes 1544 | tf_op jit(solution)/shard_map/ppermute | solution.py:393
  5.1 0.5 slice.6
  5.7 0.3 collective-permute-done.1
  6.0 0.6 %while.10 = (s32[]{:T(128)}, f32[16,128]{1,0:T(8,128)S(1)}, s32[]{:T(128)}, f32[16,128]{1,0:T(8,128)S(1)}, s32[8,128]{1,0:T(8,128)S(1)}, /*index=5*/s32[]{:T(128)}) while((s32[]{:T(128)}, f32[16,128]{1,0:T(8,128)S(1)}, s32[]{:T(128)}, f32[16,128]{1,0:T(8,128)S(1)}, s32[8,128]{1,0:T(8,128)S(1)}, /*index=5*/s32[]{:T(128)}) %tuple.24), condition=%wide.region_1.0_spmd, body=%wide.region_0.0_spmd.sunk | while | flops 130 | bytes 544945 | solution.py:449
  6.6 24.2 %all_to_all.16 = f32[128,1,128]{2,1,0:T(1,128)S(1)} all-to-all(f32[128,1,128]{2,1,0:T(1,128)S(1)} %broadcast_in_dim.32), channel_id=1, replica_groups=mesh['x'=4,'y'=4,'z'=8,'c'=2] {'x','y','z'}, dimensions={0} | all-to-all | bytes 131072 | tf_op jit(solution)/shard_map/all_to_all | solution.py:389
  30.8 5.2 %factor_columns.1 = (f32[128,4096]{1,0:T(8,128)S(1)}, f32[32,128]{1,0:T(8,128)S(1)}, f32[1,128]{1,0:T(1,128)S(1)}) custom-call(f32[128,128]{1,0:T(8,128)S(1)} %bitcast.21, f32[16,128]{1,0:T(8,128)S(1)} %get-tuple-element.47.extra_ref, f32[8,4096]{1,0:T(8,128)S(1)} %get-tuple-element.48.scaled_ref, f32[32,128]{1,0:T(8,128)S(1)} %get-tuple-element.49.noise_ref, ...), custom_call_target="tpu_custom_call" | custom-call | tf_op jit(solution)/shard_map/factor_columns/pallas_call | solution.py:335
  36.0 1.8 %collective-permute-start.2 = (f32[1,128]{1,0:T(1,128)S(1)}, f32[1,128]{1,0:T(1,128)S(1)}, u32[]{:S(2)}, u32[]{:S(2)}) collective-permute-start(f32[1,128]{1,0:T(1,128)S(1)} %get-tuple-element.50), channel_id=1, source_target_pairs={{0,1},{1,0},{2,3},{3,2},{4,5},{5,4},{6,7},{7,6},{8,9},{9,8},{10,11... | collective-permute-start | bytes 1544 | tf_op jit(solution)/shard_map/ppermute | solution.py:393
  37.8 1.4 %store_factor.1 = (f32[128,4096]{1,0:T(8,128)}, f32[32,128]{1,0:T(8,128)}) custom-call(f32[128,4096]{1,0:T(8,128)S(1)} %get-tuple-element.51.factor_ref, f32[32,128]{1,0:T(8,128)S(1)} %get-tuple-element.52.resid_ref), custom_call_target="tpu_custom_call" | custom-call | flops 4000000000 | bytes 4194304 | tf_op jit(solution)/shard_map/store_factor/pallas_call | solution.py:375
  39.2 0.0 collective-permute-done.2
  39.3 16.2 %all_to_all.17 = f32[128,1,128]{2,1,0:T(1,128)S(1)} all-to-all(f32[128,1,128]{2,1,0:T(1,128)S(1)} %broadcast_in_dim.35), channel_id=1, replica_groups=mesh['x'=4,'y'=4,'z'=8,'c'=2] {'x','y','z'}, dimensions={0} | all-to-all | bytes 131072 | tf_op jit(solution)/shard_map/all_to_all | solution.py:389
  55.5 0.5 slice_bitcast_fusion
  (6 shorter events, 0.1 us)
Async XLA Ops:
  1.9 4.1 %collective-permute-start.1 = (f32[1,128]{1,0:T(1,128)S(1)}, f32[1,128]{1,0:T(1,128)S(1)}, u32[]{:S(2)}, u32[]{:S(2)}) collective-permute-start(f32[1,128]{1,0:T(1,128)S(1)} %get-tuple-element.44), channel_id=1, source_target_pairs={{0,1},{1,0},{2,3},{3,2},{4,5},{5,4},{6,7},{7,6},{8,9},{9,8},{10,11... | collective-permute-start | bytes 1544 | tf_op jit(solution)/shard_map/ppermute | solution.py:393
  36.0 3.2 %collective-permute-start.2 = (f32[1,128]{1,0:T(1,128)S(1)}, f32[1,128]{1,0:T(1,128)S(1)}, u32[]{:S(2)}, u32[]{:S(2)}) collective-permute-start(f32[1,128]{1,0:T(1,128)S(1)} %get-tuple-element.50), channel_id=1, source_target_pairs={{0,1},{1,0},{2,3},{3,2},{4,5},{5,4},{6,7},{7,6},{8,9},{9,8},{10,11... | collective-permute-start | bytes 1544 | tf_op jit(solution)/shard_map/ppermute | solution.py:393
